TPU v7x, 256 devices: a whole 4x4x8 slice. The times are simulated.
256 devices in a mesh: lon: 16 (over y_lo, z), lat: 16 (over y_hi, x, core).
Axes of the slice: x: 4, y: 4 (y_hi: 2, y_lo: 2; y = y_hi * 2 + y_lo), z: 8, core: 2. Of those that a mesh axis runs over, the one named last changes fastest.
Arguments:
- fields_in: bfloat16 [2, 192, 384, 512], P(None, 'lat', 'lon'), may hold values from -6 to 6
- level_map: int32 [2, 192, 384], P(None, 'lat', 'lon'), may hold values from 0 to 12
- land_sea: int32 [192, 384], P('lat', 'lon'), may hold values 0 or 1
- level_table: bfloat16 [13, 512], replicated, may hold values from -4 to 4
- surface_table: bfloat16 [2, 512], replicated, may hold values from -4 to 4
- norm_gain: bfloat16 [512], replicated, may hold values from 0.25 to 1.75
- w_qkv: bfloat16 [512, 1536], replicated, may hold values from -1 to 1
- w_proj: bfloat16 [512, 512], replicated, may hold values from -0.25 to 0.25
- merge_gain: bfloat16 [2048], replicated, may hold values from 0.25 to 1.75
- w_merge: bfloat16 [2048, 1024], replicated, may hold values from -0.125 to 0.125
- coarse_gain: bfloat16 [1024], replicated, may hold values from 0.25 to 1.75
- w_in: bfloat16 [1024, 4096], P(None, 'lat'), may hold values from -0.1875 to 0.1875
- w_out: bfloat16 [4096, 1024], P('lat'), may hold values from -0.09375 to 0.09375
- w_expand: bfloat16 [1024, 2048], replicated, may hold values from -0.1875 to 0.1875
- cotangent: bfloat16 [2, 192, 384, 512], P(None, 'lat', 'lon'), may hold values from -6 to 6
Outputs:
- fields_out: bfloat16 [2, 192, 384, 512], P(None, 'lat', 'lon')
- grad_in: float32 [1024, 4096], P('lon', 'lat')
- grad_out: float32 [4096, 1024], P('lat', 'lon')
All inputs are finite; a program needn't handle non-finite values. No bound on the sum of `land_sea` on one device may be relied on, other than what follows from the above.
Results may differ from a plain program's by a relative error of at most 0.025.
Values may be sent and summed in bfloat16 or wider, within the bound.
No kernel may reach another device: no remote copies, remote signals or barrier semaphores. Data moves between devices by JAX's collectives and lax.ppermute only.
A program may use at most 128 MiB of HBM per device.

v0:
```python
import math

import jax
import jax.numpy as jnp
import numpy as np
from jax import lax
from jax.experimental import pallas as pl
from jax.experimental.pallas import tpu as pltpu
from jax.sharding import PartitionSpec as P


WIN_LON = 6
SHIFT_LON = 3
EPSILON = 1e-05

LEVELS, ROWS, COLS, C1 = 2, 12, 24, 512
TOKENS = LEVELS * ROWS * COLS
HALF = TOKENS // 2
COARSE = TOKENS // 4
EDGE = 48
C2 = 1024
FB = 256
F32 = jnp.float32
BF16 = jnp.bfloat16


def token_tables():
    natural_to_merge = np.zeros(TOKENS, np.int32)
    half_to_edge = np.full(HALF, -1, np.int32)
    edge_to_half = {}
    source_to_window = np.full(2 * HALF + 2 * EDGE, -1, np.int32)
    for level in range(LEVELS):
        for row in range(ROWS):
            for col in range(COLS):
                q = (col % 2) * 2 + row % 2
                h, i3, j = row // 6, row % 6 // 2, col // 2
                merge = q * COARSE + h * 72 + level * 36 + i3 * 12 + j
                natural_to_merge[(level * ROWS + row) * COLS + col] = merge
                if h == 0:
                    place = q * 72 + level * 36 + i3 * 12 + j
                    if col < SHIFT_LON:
                        half_to_edge[place] = level * 18 + row * 3 + col
                        edge_to_half[level * 18 + row * 3 + col] = merge
    for level in range(LEVELS):
        for r in range(ROWS):
            for c in range(COLS):
                window = (c // WIN_LON) * 144 + level * 72 + r * 6 + c % WIN_LON
                row, col = r % 6, c + SHIFT_LON
                if col < COLS:
                    q = (col % 2) * 2 + row % 2
                    place = q * 72 + level * 36 + row // 2 * 12 + col // 2
                    source = place + (HALF if r >= 6 else 0)
                else:
                    source = 2 * HALF + level * 18 + row * 3 + col - COLS
                    source += EDGE if r >= 6 else 0
                source_to_window[source] = window
    window_to_source = np.zeros(TOKENS, np.int32)
    for source, window in enumerate(source_to_window):
        if window >= 0:
            window_to_source[window] = source
    merge_to_natural = np.zeros(TOKENS, np.int32)
    merge_to_natural[natural_to_merge] = np.arange(TOKENS, dtype=np.int32)
    edges_to_merge = np.full(2 * EDGE, -1, np.int32)
    for edge, merge in edge_to_half.items():
        edges_to_merge[edge] = merge + 72
        edges_to_merge[EDGE + edge] = merge
    return natural_to_merge, merge_to_natural, half_to_edge, source_to_window, window_to_source, edges_to_merge


N2M, M2N, H2E, S2W, W2S, E2M = token_tables()


def lanes(table):
    return jnp.asarray(table.reshape(1, -1))


def picks(rows, table):
    spots = lax.broadcasted_iota(jnp.int32, (rows, table.shape[1]), 0)
    return (spots == table).astype(F32).astype(BF16)


def mm(a, b):
    return jnp.dot(a, b, preferred_element_type=F32)


def mm_nt(a, b):
    return lax.dot_general(a, b, (((1,), (1,)), ((), ())), preferred_element_type=F32)


def mm_tn(a, b):
    return lax.dot_general(a, b, (((0,), (0,)), ((), ())), preferred_element_type=F32)


def normed_rows(values, gain):
    center = values - jnp.mean(values, axis=-1, keepdims=True)
    spread = jnp.mean(center * center, axis=-1, keepdims=True)
    return center * lax.rsqrt(spread + EPSILON) * gain


def front_kernel(
    fin, ids, level_table, surface_table, gain, n2m, h2e,
    fields_out, up_out, lo_out, lon_out, diag_out, table,
):
    table[...] = jnp.zeros_like(table)
    table[0:13, :] = level_table[...].astype(F32)
    table[13:15, :] = surface_table[...].astype(F32)
    order = picks(TOKENS, n2m[...])
    spots = lax.broadcasted_iota(jnp.int32, (16, TOKENS), 0)
    hot = ((spots == ids[0:1, :]) | (spots == ids[1:2, :])).astype(F32).astype(BF16)
    fields = mm(order, fin[...]) + mm(mm_nt(order, hot).astype(BF16), table[...].astype(BF16))
    fields_out[...] = fields
    normed = normed_rows(fields, gain[...].astype(F32))
    up = jnp.concatenate([normed[q * COARSE : q * COARSE + 72] for q in range(4)], axis=0).astype(BF16)
    lo = jnp.concatenate([normed[q * COARSE + 72 : (q + 1) * COARSE] for q in range(4)], axis=0).astype(BF16)
    up_out[...] = up
    lo_out[...] = lo
    edge = picks(EDGE, h2e[...])
    lon_out[...] = mm(edge, lo).astype(BF16)
    diag_out[...] = mm(edge, up).astype(BF16)


def attention_kernel(flag, lo, up, lon, diag, w_qkv, s2w, w2s, lo_out, up_out, lon_out, diag_out, src, qkv, att):
    src[0:HALF, :] = lo[...]
    src[HALF : 2 * HALF, :] = up[...]
    src[2 * HALF : 2 * HALF + EDGE, :] = lon[...]
    src[2 * HALF + EDGE :, :] = diag[...]
    windows = mm(picks(TOKENS, s2w[...]), src[...]).astype(BF16)
    qkv[...] = mm(windows, w_qkv[...]).astype(BF16)
    size = 144
    top = lax.broadcasted_iota(jnp.int32, (size, size), 0)
    left = lax.broadcasted_iota(jnp.int32, (size, size), 1)

    def low(t):
        return ((t >= 36) & (t < 72)) | (t >= 108)

    apart = (low(top) != low(left)) & (flag[0] == 1)
    lane = lax.broadcasted_iota(jnp.int32, (size, 128), 1)
    first = lane < 64
    ones = [jnp.where(first, 1.0, 0.0).astype(BF16), jnp.where(first, 0.0, 1.0).astype(BF16)]

    def one_window(w, carry):
        rows = pl.ds(pl.multiple_of(w * size, 16), size)
        for pair in range(4):
            cols = pair * 128
            queries = qkv[rows, cols : cols + 128]
            keys = qkv[rows, C1 + cols : C1 + cols + 128]
            values = qkv[rows, 2 * C1 + cols : 2 * C1 + cols + 128]
            total = None
            for side in range(2):
                scores = mm_nt(queries * ones[side], keys) * (1.0 / math.sqrt(64))
                scores = jnp.where(apart, -1e30, scores)
                peak = jnp.max(scores, axis=-1, keepdims=True)
                probs = jnp.exp(scores - peak).astype(BF16)
                both = mm(probs, jnp.concatenate([values * ones[side], ones[side]], axis=1))
                total = both if total is None else total + both
            att[rows, cols : cols + 128] = (total[:, :128] / total[:, 128:]).astype(BF16)
        return carry

    lax.fori_loop(0, 4, one_window, 0)
    back = mm(picks(2 * HALF + 2 * EDGE, w2s[...]), att[...]).astype(BF16)
    lo_out[...] = back[0:HALF]
    up_out[...] = back[HALF : 2 * HALF]
    lon_out[...] = back[2 * HALF : 2 * HALF + EDGE]
    diag_out[...] = back[2 * HALF + EDGE :]


def merge_kernel(
    lo, up, lon, diag, fields, w_proj, merge_gain, w_merge, coarse_gain, e2m, skip_out, coarse_out, cn_out
):
    upper, lower = up[...].astype(F32), lo[...].astype(F32)
    parts = []
    for q in range(4):
        parts.append(upper[q * 72 : (q + 1) * 72])
        parts.append(lower[q * 72 : (q + 1) * 72])
    edges = jnp.concatenate([lon[...], diag[...]], axis=0)
    attended = (jnp.concatenate(parts, axis=0) + mm(picks(TOKENS, e2m[...]), edges)).astype(BF16)
    skip = (fields[...] + mm(attended, w_proj[...])).astype(BF16)
    skip_out[...] = skip
    skip = skip.astype(F32)
    blocks = [skip[q * COARSE : (q + 1) * COARSE] for q in range(4)]
    mean = sum(jnp.sum(b, axis=-1, keepdims=True) for b in blocks) * (1.0 / (4 * C1))
    blocks = [b - mean for b in blocks]
    spread = sum(jnp.sum(b * b, axis=-1, keepdims=True) for b in blocks) * (1.0 / (4 * C1))
    scale = lax.rsqrt(spread + EPSILON)
    coarse = None
    for q in range(4):
        gain = merge_gain[0:1, q * C1 : (q + 1) * C1].astype(F32)
        part = mm((blocks[q] * scale * gain).astype(BF16), w_merge[q * C1 : (q + 1) * C1, :])
        coarse = part if coarse is None else coarse + part
    coarse = coarse.astype(BF16)
    coarse_out[...] = coarse
    cn_out[...] = normed_rows(coarse.astype(F32), coarse_gain[...].astype(F32)).astype(BF16)


def cotangent_kernel(cot, w_expand, n2m, dc_out, ordered, total):
    ordered[...] = mm(picks(TOKENS, n2m[...]), cot[...]).astype(BF16)
    total[...] = jnp.zeros_like(total)

    def one_place(q, carry):
        rows = pl.ds(pl.multiple_of(q * COARSE, 16), COARSE)
        cols = pl.ds(pl.multiple_of(q * C1, C1), C1)
        total[...] += mm_nt(ordered[rows, :], w_expand[:, cols])
        return carry

    lax.fori_loop(0, 4, one_place, 0)
    dc_out[...] = total[...].astype(BF16)


NEAR = 80
QUAD = 4 * COARSE


def stack_into(full, refs):
    at = 0
    for ref in refs:
        full[at : at + ref.shape[0], :] = ref[...]
        at += ref.shape[0]


def hidden_rows(full, w_in, w_in_far, w_out, w_out_far, hidden_out, slope_out, partial):
    root = math.sqrt(2.0 / math.pi)

    def one_part(k, carry):
        rows = pl.ds(pl.multiple_of(k * (QUAD // 2), 32), QUAD // 2)
        total = None
        for side, (win, wout) in enumerate(((w_in, w_out), (w_in_far, w_out_far))):
            x = mm(full[rows, :], win[...])
            t = jnp.tanh(root * (x + 0.044715 * (x * x * x)))
            half = 0.5 * (1.0 + t)
            hidden = (x * half).astype(BF16)
            slope = half + 0.5 * x * (1.0 - t * t) * (root * (1.0 + 3 * 0.044715 * (x * x)))
            cols = slice(side * FB, (side + 1) * FB)
            hidden_out[rows, cols] = hidden
            slope_out[rows, cols] = slope.astype(BF16)
            part = mm(hidden, wout[...])
            total = part if total is None else total + part
        partial[rows, :] = total.astype(BF16)
        return carry

    lax.fori_loop(0, 2, one_part, 0)


def near_kernel(own, far, right, left, w_in, w_in_far, w_out, w_out_far, partial, full, hidden, slope):
    stack_into(full, (own, far, right, left))
    hidden_rows(full, w_in, w_in_far, w_out, w_out_far, hidden, slope, partial)


def wide_kernel(
    right, left, far_right2, far_left2, w_in, w_in_far, w_out, w_out_far,
    near_right, near_left, send_right, send_left, full, hidden, slope, partial,
):
    full[0:NEAR, :] = right[0:NEAR, :]
    full[NEAR:COARSE, :] = left[0 : COARSE - NEAR, :]
    full[COARSE : 2 * COARSE, :] = right[NEAR:, :]
    full[2 * COARSE : 3 * COARSE, :] = left[COARSE - NEAR :, :]
    full[3 * COARSE : 3 * COARSE + NEAR, :] = far_right2[...]
    full[3 * COARSE + NEAR :, :] = far_left2[...]
    hidden_rows(full, w_in, w_in_far, w_out, w_out_far, hidden, slope, partial)
    near_right[...] = partial[2 * COARSE : 3 * COARSE, :]
    near_left[...] = partial[COARSE : 2 * COARSE, :]
    send_right[0:NEAR, :] = partial[0:NEAR, :]
    send_right[NEAR:, :] = partial[3 * COARSE : 3 * COARSE + NEAR, :]
    send_left[0 : COARSE - NEAR, :] = partial[NEAR:COARSE, :]
    send_left[COARSE - NEAR :, :] = partial[3 * COARSE + NEAR :, :]


def added(x, y):
    return (x.astype(F32) + y.astype(F32)).astype(BF16)


def pass_kernel(near, far_right, far_left, got_right, got_left, own_r, own_l, far_r, far_l):
    rest = COARSE - NEAR
    own_r[0:NEAR, :] = added(near[3 * COARSE : 3 * COARSE + NEAR, :], got_right[0:NEAR, :])
    own_r[NEAR:, :] = near[3 * COARSE + NEAR :, :]
    own_l[0:NEAR, :] = near[2 * COARSE : 2 * COARSE + NEAR, :]
    own_l[NEAR:, :] = added(near[2 * COARSE + NEAR : 3 * COARSE, :], got_left[0:rest, :])
    far_r[0:NEAR, :] = added(far_right[0:NEAR, :], got_right[NEAR:, :])
    far_r[NEAR:, :] = far_right[NEAR:, :]
    far_l[0:NEAR, :] = far_left[0:NEAR, :]
    far_l[NEAR:, :] = added(far_left[NEAR:, :], got_left[rest:, :])


def far_kernel(near, got_right, got_left, send):
    total = near[COARSE : 2 * COARSE, :].astype(F32) + got_right[...].astype(F32)
    send[...] = (total + got_left[...].astype(F32)).astype(BF16)


def gradient_kernel(
    own, far, right, left, right2, left2, far_right2, far_left2, near_full, near_hidden, near_slope,
    wide_full, wide_hidden, wide_slope, w_out, w_out_far, in_own, in_far, out_own, out_far, dfull, dact,
):
    stack_into(dfull, (own, far, right, left))
    dfull[QUAD : QUAD + NEAR, :] = right2[0:NEAR, :]
    dfull[QUAD + NEAR : QUAD + COARSE, :] = left2[0 : COARSE - NEAR, :]
    dfull[QUAD + COARSE : QUAD + 2 * COARSE, :] = right2[NEAR:, :]
    dfull[QUAD + 2 * COARSE : QUAD + 3 * COARSE, :] = left2[COARSE - NEAR :, :]
    dfull[QUAD + 3 * COARSE : QUAD + 3 * COARSE + NEAR, :] = far_right2[...]
    dfull[QUAD + 3 * COARSE + NEAR :, :] = far_left2[...]
    for side, wout in enumerate((w_out, w_out_far)):
        cols = slice(side * FB, (side + 1) * FB)
        for part, slope in enumerate((near_slope, wide_slope)):
            rows = slice(part * QUAD, (part + 1) * QUAD)
            back = mm_nt(dfull[rows, :], wout[...])
            dact[rows, cols] = (back * slope[:, cols].astype(F32)).astype(BF16)

    def one_block(k, carry):
        c = pl.ds(pl.multiple_of(k * 256, 256), 256)
        both = mm_tn(dfull[0:QUAD, c], near_hidden[...]) + mm_tn(dfull[QUAD:, c], wide_hidden[...])
        out_own[c, :] = both[:, :FB].astype(BF16)
        out_far[c, :] = both[:, FB:].astype(BF16)
        both = mm_tn(near_full[:, c], dact[0:QUAD, :]) + mm_tn(wide_full[:, c], dact[QUAD:, :])
        in_own[c, :] = both[:, :FB].astype(BF16)
        in_far[c, :] = both[:, FB:].astype(BF16)
        return carry

    lax.fori_loop(0, 4, one_block, 0)


def expand_kernel(coarse, near, got_right, got_left, got_far, w_expand, skip, m2n, fields_out, parts):
    mixed = near[0:COARSE, :].astype(F32) + got_right[...].astype(F32)
    mixed = mixed + (got_left[...].astype(F32) + got_far[...].astype(F32))
    coarse_out = (coarse[...].astype(F32) + mixed).astype(BF16)

    def one_place(q, carry):
        rows = pl.ds(pl.multiple_of(q * COARSE, 16), COARSE)
        cols = pl.ds(pl.multiple_of(q * C1, C1), C1)
        parts[rows, :] = (skip[rows, :].astype(F32) + mm(coarse_out, w_expand[:, cols])).astype(BF16)
        return carry

    lax.fori_loop(0, 4, one_place, 0)
    fields_out[...] = mm(picks(TOKENS, m2n[...]), parts[...]).astype(BF16)


def shaped(dims, dtype=BF16):
    return jax.ShapeDtypeStruct(dims, dtype)


def run(kernel, outs, args, flops, scratch=(), smem=()):
    nbytes = sum(a.size * a.dtype.itemsize for a in args) + sum(math.prod(o.shape) * 2 for o in outs)
    return pl.pallas_call(
        kernel,
        out_shape=tuple(outs),
        in_specs=[pl.BlockSpec(memory_space=pltpu.SMEM if k in smem else pltpu.VMEM) for k in range(len(args))],
        out_specs=tuple(pl.BlockSpec(memory_space=pltpu.VMEM) for _ in outs),
        scratch_shapes=list(scratch),
        compiler_params=pltpu.CompilerParams(vmem_limit_bytes=32 * 1024 * 1024),
        cost_estimate=pl.CostEstimate(flops=int(flops), bytes_accessed=int(nbytes), transcendentals=0),
    )(*args)


def lat_of(y, x, core):
    return (y % 2) * 8 + (x % 4) * 2 + core % 2


def lat_moves(dy, dx, dcore):
    return [(l, lat_of(l // 8 + dy, l // 2 % 4 + dx, l % 2 + dcore)) for l in range(16)]


def on_lat(value, dy=0, dx=0, dcore=0):
    return lax.ppermute(value, "lat", lat_moves(dy, dx, dcore))


def shift(value, axes, steps):
    if axes == "both":
        pairs = [
            (o * 16 + l, (o + steps) % 16 * 16 + (l + steps) % 16) for o in range(16) for l in range(16)
        ]
        return lax.ppermute(value, ("lon", "lat"), pairs)
    return lax.ppermute(value, axes, [(s, (s + steps) % 16) for s in range(16)])


def gathered(block):
    far = on_lat(block, dy=1)
    right, left = on_lat(block, dx=1), on_lat(block, dx=-1)
    right2 = on_lat(jnp.concatenate([right[:NEAR], far], axis=0), dx=1)
    left2 = on_lat(jnp.concatenate([left[NEAR:], far], axis=0), dx=-1)
    far_right2, far_left2 = on_lat(right2[NEAR : 2 * NEAR], dx=1), on_lat(left2[COARSE:], dx=-1)
    return (block, far, right, left), (right2, left2, far_right2, far_left2)


EIGHTS = [[half * 8 + z for z in range(8)] for half in range(2)]


def whole(
    fields_in, level_map, land_sea, level_table, surface_table, norm_gain, w_qkv, w_proj, merge_gain,
    w_merge, coarse_gain, w_in, w_out, w_expand, cotangent,
):
    lat, lon_index = lax.axis_index("lat"), lax.axis_index("lon")
    surface = 13 + (land_sea == 1).astype(jnp.int32)
    ids = jnp.concatenate([level_map.reshape(2 * ROWS, COLS), surface, surface], axis=0).reshape(2, TOKENS)
    w_in_far, w_out_far = on_lat(w_in, dcore=1), on_lat(w_out, dcore=1)
    fields, up, lo, lon, diag = run(
        front_kernel,
        [shaped((TOKENS, C1), F32), shaped((HALF, C1)), shaped((HALF, C1)), shaped((EDGE, C1)), shaped((EDGE, C1))],
        (
            fields_in.reshape(TOKENS, C1), ids,
            level_table, surface_table, norm_gain.reshape(1, C1), lanes(N2M), lanes(H2E),
        ),
        4e8,
        [pltpu.VMEM((16, C1), F32)],
    )
    up, lon, diag = shift(up, "lat", -1), shift(lon, "lon", -1), shift(diag, "both", -1)
    (dc,) = run(
        cotangent_kernel, [shaped((COARSE, C2))], (cotangent.reshape(TOKENS, C1), w_expand, lanes(N2M)), 1e9,
        [pltpu.VMEM((TOKENS, C1), BF16), pltpu.VMEM((COARSE, C2), F32)],
    )
    dc_near, dc_wide = gathered(dc)
    flag = (lat == 15).astype(jnp.int32).reshape(1)
    lo, up, lon, diag = run(
        attention_kernel,
        [shaped((HALF, C1)), shaped((HALF, C1)), shaped((EDGE, C1)), shaped((EDGE, C1))],
        (flag, lo, up, lon, diag, w_qkv, lanes(S2W), lanes(W2S)),
        3e9,
        [pltpu.VMEM((2 * HALF + 2 * EDGE, C1), BF16), pltpu.VMEM((TOKENS, 3 * C1), BF16), pltpu.VMEM((TOKENS, C1), BF16)],
        smem=(0,),
    )
    up, lon, diag = shift(up, "lat", 1), shift(lon, "lon", 1), shift(diag, "both", 1)
    skip, coarse, cn = run(
        merge_kernel,
        [shaped((TOKENS, C1)), shaped((COARSE, C2)), shaped((COARSE, C2))],
        (lo, up, lon, diag, fields, w_proj, merge_gain.reshape(1, 4 * C1), w_merge, coarse_gain.reshape(1, C2), lanes(E2M)),
        2e9,
    )
    cn_near, cn_wide = gathered(cn)
    weights = (w_in, w_in_far, w_out, w_out_far)
    kept = [shaped((QUAD, C2)), shaped((QUAD, 2 * FB)), shaped((QUAD, 2 * FB))]
    near, *near_kept = run(near_kernel, [shaped((QUAD, C2)), *kept], (*cn_near, *weights), 2.5e9)
    far_right, far_left, to_right, to_left, *wide_kept = run(
        wide_kernel,
        [shaped((COARSE, C2)), shaped((COARSE, C2)), shaped((2 * NEAR, C2)), shaped((2 * (COARSE - NEAR), C2)), *kept],
        (*cn_wide, *weights),
        2.5e9,
        [pltpu.VMEM((QUAD, C2), BF16)],
    )
    got_right, got_left = on_lat(to_right, dx=1), on_lat(to_left, dx=-1)
    in_own, in_far, out_own, out_far = run(
        gradient_kernel,
        [shaped((C2, FB))] * 4,
        (*dc_near, *dc_wide, *near_kept, *wide_kept, w_out, w_out_far),
        4e9,
        [pltpu.VMEM((8 * COARSE, C2), BF16), pltpu.VMEM((8 * COARSE, 2 * FB), BF16)],
    )
    own_r, own_l, far_r, far_l = run(
        pass_kernel, [shaped((COARSE, C2))] * 4, (near, far_right, far_left, got_right, got_left), 1e8
    )
    far_r, far_l = on_lat(far_r, dx=1), on_lat(far_l, dx=-1)
    own_r, own_l = on_lat(own_r, dx=1), on_lat(own_l, dx=-1)
    (across,) = run(far_kernel, [shaped((COARSE, C2))], (near, far_r, far_l), 1e8)
    across = on_lat(across, dy=1)

    out_sum, in_sum = added(out_own, on_lat(out_far, dcore=1)), added(in_own, on_lat(in_far, dcore=1))
    both = jnp.stack([out_sum.reshape(2, 8, 64, FB), in_sum.reshape(2, 8, 64, FB)], axis=2)
    side = lon_index // 8
    mine = lax.dynamic_index_in_dim(both, side, 0, keepdims=False)
    other = lax.dynamic_index_in_dim(both, 1 - side, 0, keepdims=False)
    other = lax.ppermute(other, "lon", [(o, (o + 8) % 16) for o in range(16)])
    pieces = lax.all_to_all(added(mine, other), "lon", 0, 0, axis_index_groups=EIGHTS, tiled=True)
    total = jnp.sum(pieces.astype(F32), axis=0)
    grad_out, grad_in = total[0].T, total[1]
    (fields_out,) = run(
        expand_kernel,
        [shaped((TOKENS, C1))],
        (coarse, near, own_r, own_l, across, w_expand, skip, lanes(M2N)),
        1e9,
        [pltpu.VMEM((TOKENS, C1), BF16)],
    )
    return (fields_out.reshape(LEVELS, ROWS, COLS, C1), grad_in, grad_out)


def solution(mesh):
    placed = (
        P(None, "lat", "lon", None),
        P(None, "lat", "lon"),
        P("lat", "lon"),
        P(),
        P(),
        P(),
        P(),
        P(),
        P(),
        P(),
        P(),
        P(None, "lat"),
        P("lat", None),
        P(),
        P(None, "lat", "lon", None),
    )
    return jax.shard_map(
        whole,
        mesh=mesh,
        in_specs=placed,
        out_specs=(P(None, "lat", "lon", None), P("lon", "lat"), P("lat", "lon")),
        check_vma=False,
    )
```

profile of v0, /device:TPU:6, one launch (start us, length us, event | category | flops | bytes accessed | tf_op | source)
XLA Modules:
  0.0 154.9 jit_solution(12797491685138179085)
XLA Ops:
  0.7 0.8 convert_add_fusion.1
  3.6 1.1 copy-done.14
  4.7 0.7 copy-done.19
  6.7 1.6 %shard_map.229 = (f32[576,512]{1,0:T(8,128)S(1)}, bf16[288,512]{1,0:T(8,128)(2,1)S(1)}, bf16[288,512]{1,0:T(8,128)(2,1)S(1)}, bf16[48,512]{1,0:T(8,128)(2,1)S(1)}, bf16[48,512]{1,0:T(8,128)(2,1)S(1)}) custom-call(bf16[576,512]{1,0:T(8,128)(2,1)S(1)} %bitcast.24, s32[2,576]{1,0:T(2,128)S(1)} %reshape.41.ids, bf16[13,512]{1,0:T(8,128)(2,1)S(1)} %copy-done.19, ...), custom_call_target="tpu_custom_call" | custom-call | flops 400000000 | bytes 1892224 | tf_op jit(solution)/shard_map/pallas_call | solution.py:340
  8.3 1.0 copy-done.25
  10.4 6.9 %collective-permute-start.1 = (bf16[48,512]{1,0:T(8,128)(2,1)S(1)}, bf16[48,512]{1,0:T(8,128)(2,1)S(1)}, u32[]{:S(2)}, u32[]{:S(2)}) collective-permute-start(bf16[48,512]{1,0:T(8,128)(2,1)S(1)} %get-tuple-element.36), channel_id=1, source_target_pairs={{0,240},{16,0},{32,16},{48,32},{64,48},{80,64},{96,80},{112,96},{1... | collective-permute-start | bytes 147464 | tf_op jit(solution)/shard_map/ppermute | solution.py:369
  17.2 0.8 collective-permute-start.2
  18.1 2.2 %copy-done = bf16[1024,2048]{1,0:T(8,128)(2,1)S(1)} copy-done((bf16[1024,2048]{1,0:T(8,128)(2,1)S(1)}, bf16[1024,2048]{1,0:T(8,128)(2,1)}, u32[]{:S(2)}) %copy-start) | copy-done | bytes 4194328
  20.3 2.6 %shard_map.237.own = bf16[144,1024]{1,0:T(8,128)(2,1)S(1)} custom-call(bf16[576,512]{1,0:T(8,128)(2,1)S(1)} %bitcast.23, bf16[1024,2048]{1,0:T(8,128)(2,1)S(1)} %copy-done, s32[1,576]{1,0:T(1,128)S(1)} %copy-done.11), custom_call_target="tpu_custom_call" | custom-call | flops 1000000000 | bytes 5081344 | tf_op jit(solution)/shard_map/pallas_call | solution.py:340
  23.5 1.0 copy-done.28
  24.5 5.2 %shard_map.230 = (bf16[288,512]{1,0:T(8,128)(2,1)S(1)}, bf16[288,512]{1,0:T(8,128)(2,1)S(1)}, bf16[48,512]{1,0:T(8,128)(2,1)S(1)}, bf16[48,512]{1,0:T(8,128)(2,1)S(1)}) custom-call(s32[1]{0:T(128)} %bitcast.flag, bf16[288,512]{1,0:T(8,128)(2,1)S(1)} %copy-done.28, bf16[288,512]{1,0:T(8,128)(2,1)S(1)} %collective-permute-done.up, ...), custom_call_target="tpu_custom_call" | custom-call | flops 3000000000 | bytes 2954116 | tf_op jit(solution)/shard_map/pallas_call | solution.py:340
  29.7 2.1 %collective-permute-start.3 = (bf16[288,512]{1,0:T(8,128)(2,1)S(1)}, bf16[288,512]{1,0:T(8,128)(2,1)S(1)}, u32[]{:S(2)}, u32[]{:S(2)}) collective-permute-start(bf16[288,512]{1,0:T(8,128)(2,1)S(1)} %get-tuple-element.39), channel_id=1, source_target_pairs={{0,1},{1,2},{2,3},{3,4},{4,5},{5,6},{6,7},{7,8},{8,9},{9,10},{10,1... | collective-permute-start | bytes 884744 | tf_op jit(solution)/shard_map/ppermute | solution.py:369
  31.8 2.6 %collective-permute-start.22 = (bf16[144,1024]{1,0:T(8,128)(2,1)S(1)}, bf16[144,1024]{1,0:T(8,128)(2,1)S(1)}, u32[]{:S(2)}, u32[]{:S(2)}) collective-permute-start(bf16[144,1024]{1,0:T(8,128)(2,1)S(1)} %shard_map.237.own), channel_id=1, source_target_pairs={{0,8},{1,9},{2,10},{3,11},{4,12},{5,13},{6,14},{7,15},{8,0},{9,1},... | collective-permute-start | bytes 884744 | tf_op jit(solution)/shard_map/ppermute | solution.py:360
  34.4 3.1 %collective-permute-start.5 = (bf16[48,512]{1,0:T(8,128)(2,1)S(1)}, bf16[48,512]{1,0:T(8,128)(2,1)S(1)}, u32[]{:S(2)}, u32[]{:S(2)}) collective-permute-start(bf16[48,512]{1,0:T(8,128)(2,1)S(1)} %get-tuple-element.41), channel_id=1, source_target_pairs={{0,17},{1,18},{2,19},{3,20},{4,21},{5,22},{6,23},{7,24},{8,25},{9,... | collective-permute-start | bytes 147464 | tf_op jit(solution)/shard_map/ppermute | solution.py:368
  37.8 3.0 %collective-permute-done.4.lon = bf16[48,512]{1,0:T(8,128)(2,1)S(1)} collective-permute-done((bf16[48,512]{1,0:T(8,128)(2,1)S(1)}, bf16[48,512]{1,0:T(8,128)(2,1)S(1)}, u32[]{:S(2)}, u32[]{:S(2)}) %collective-permute-start.4) | collective-permute-done | bytes 49184 | tf_op jit(solution)/shard_map/ppermute | solution.py:369
  40.8 0.8 collective-permute-done.5.diag
  41.7 1.9 %shard_map.231 = (bf16[576,512]{1,0:T(8,128)(2,1)S(1)}, bf16[144,1024]{1,0:T(8,128)(2,1)S(1)}, bf16[144,1024]{1,0:T(8,128)(2,1)S(1)}) custom-call(bf16[288,512]{1,0:T(8,128)(2,1)S(1)} %get-tuple-element.38.lo, bf16[288,512]{1,0:T(8,128)(2,1)S(1)} %collective-permute-done.3.up, bf16[48,512]{1,0:T(8,128)(2,1)S(1)} %collective-permute-done.4.lon, ...), custom_call_target="tpu_custom_call" | custom-call | flops 2000000000 | bytes 7772544 | tf_op jit(solution)/shard_map/pallas_call | solution.py:340
  44.2 4.9 %collective-permute-start.7 = (bf16[144,1024]{1,0:T(8,128)(2,1)S(1)}, bf16[144,1024]{1,0:T(8,128)(2,1)S(1)}, u32[]{:S(2)}, u32[]{:S(2)}) collective-permute-start(bf16[144,1024]{1,0:T(8,128)(2,1)S(1)} %get-tuple-element.44.own), channel_id=1, source_target_pairs={{0,2},{1,3},{2,4},{3,5},{4,6},{5,7},{6,0},{7,1},{8,10},{9,11},{10,... | collective-permute-start | bytes 884744 | tf_op jit(solution)/shard_map/ppermute | solution.py:360
  49.5 5.1 %collective-permute-done.7.right = bf16[144,1024]{1,0:T(8,128)(2,1)S(1)} collective-permute-done((bf16[144,1024]{1,0:T(8,128)(2,1)S(1)}, bf16[144,1024]{1,0:T(8,128)(2,1)S(1)}, u32[]{:S(2)}, u32[]{:S(2)}) %collective-permute-start.7) | collective-permute-done | bytes 294944 | tf_op jit(solution)/shard_map/ppermute | solution.py:360
  54.6 3.8 %collective-permute-start.25 = (bf16[224,1024]{1,0:T(8,128)(2,1)S(1)}, bf16[224,1024]{1,0:T(8,128)(2,1)S(1)}, u32[]{:S(2)}, u32[]{:S(2)}) collective-permute-start(bf16[224,1024]{1,0:T(8,128)(2,1)S(1)} %pad_maximum_fusion.1), channel_id=1, source_target_pairs={{0,2},{1,3},{2,4},{3,5},{4,6},{5,7},{6,0},{7,1},{8,10},{9,11},{10,... | collective-permute-start | bytes 1376264 | tf_op jit(solution)/shard_map/ppermute | solution.py:360
  58.4 8.8 %collective-permute-done.8.left = bf16[144,1024]{1,0:T(8,128)(2,1)S(1)} collective-permute-done((bf16[144,1024]{1,0:T(8,128)(2,1)S(1)}, bf16[144,1024]{1,0:T(8,128)(2,1)S(1)}, u32[]{:S(2)}, u32[]{:S(2)}) %collective-permute-start.8) | collective-permute-done | bytes 294944 | tf_op jit(solution)/shard_map/ppermute | solution.py:360
  67.2 1.1 collective-permute-start.11
  68.4 1.0 collective-permute-start.12
  69.5 12.5 %collective-permute-done.12.left = bf16[208,1024]{1,0:T(8,128)(2,1)S(1)} collective-permute-done((bf16[208,1024]{1,0:T(8,128)(2,1)S(1)}, bf16[208,1024]{1,0:T(8,128)(2,1)S(1)}, u32[]{:S(2)}, u32[]{:S(2)}) %collective-permute-start.12) | collective-permute-done | bytes 426016 | tf_op jit(solution)/shard_map/ppermute | solution.py:360
  82.1 2.1 %collective-permute-start.14 = (bf16[64,1024]{1,0:T(8,128)(2,1)S(1)}, bf16[64,1024]{1,0:T(8,128)(2,1)S(1)}, u32[]{:S(2)}, u32[]{:S(2)}) collective-permute-start(bf16[64,1024]{1,0:T(8,128)(2,1)S(1)} %slice.43), channel_id=1, source_target_pairs={{0,6},{1,7},{2,0},{3,1},{4,2},{5,3},{6,4},{7,5},{8,14},{9,15},{10,... | collective-permute-start | bytes 393224 | tf_op jit(solution)/shard_map/ppermute | solution.py:360
  84.2 1.5 collective-permute-start.13
  85.7 2.4 %shard_map.232 = (bf16[576,1024]{1,0:T(8,128)(2,1)S(1)}, bf16[576,1024]{1,0:T(8,128)(2,1)S(1)}, bf16[576,512]{1,0:T(8,128)(2,1)S(1)}, bf16[576,512]{1,0:T(8,128)(2,1)S(1)}) custom-call(bf16[144,1024]{1,0:T(8,128)(2,1)S(1)} %get-tuple-element.44.own, bf16[144,1024]{1,0:T(8,128)(2,1)S(1)} %collective-permute-done.6.far, ...), custom_call_target="tpu_custom_call" | custom-call | flops 2500000000 | bytes 6815744 | tf_op jit(solution)/shard_map/pallas_call | solution.py:340
  88.3 1.5 collective-permute-done.13.far_right2
  89.8 3.1 %shard_map.233 = (bf16[144,1024]{1,0:T(8,128)(2,1)S(1)}, bf16[144,1024]{1,0:T(8,128)(2,1)S(1)}, bf16[160,1024]{1,0:T(8,128)(2,1)}, bf16[128,1024]{1,0:T(8,128)(2...) custom-call(bf16[224,1024]{1,0:T(8,128)(2,1)S(1)} %collective-permute-done.11.rig, ...), custom_call_target="tpu_custom_call" | custom-call | flops 2500000000 | bytes 6815744 | tf_op jit(solution)/shard_map/pallas_call | solution.py:340
  93.6 0.7 copy-done.5
  95.1 6.3 %shard_map.238 = (bf16[1024,256]{1,0:T(8,128)(2,1)S(1)}, bf16[1024,256]{1,0:T(8,128)(2,1)}, bf16[1024,256]{1,0:T(8,128)(2,1)S(1)}, bf16[1024,256]{1,0:T(8,128)(2,1)}) custom-call(bf16[144,1024]{1,0:T(8,128)(2,1)S(1)} %shard_map.237.own, bf16[144,1024]{1,0:T(8,128)(2,1)S(1)} %collective-permute-done.22.far, ...), custom_call_target="tpu_custom_call" | custom-call | flops 4000000000 | bytes 10223616 | tf_op jit(solution)/shard_map/pallas_call | solution.py:340
  101.9 1.7 %collective-permute-done.29 = bf16[1024,256]{1,0:T(8,128)(2,1)} collective-permute-done((bf16[1024,256]{1,0:T(8,128)(2,1)}, bf16[1024,256]{1,0:T(8,128)(2,1)}, u32[]{:S(2)}, u32[]{:S(2)}) %collective-permute-start.29) | collective-permute-done | bytes 524320 | tf_op jit(solution)/shard_map/ppermute | solution.py:360
  103.6 1.2 add_convert_fusion.1
  104.8 1.4 add_convert_fusion
  106.2 1.0 fusion.2
  107.8 2.4 %collective-permute-start.15 = (bf16[160,1024]{1,0:T(8,128)(2,1)}, bf16[160,1024]{1,0:T(8,128)(2,1)S(1)}, u32[]{:S(2)}, u32[]{:S(2)}) collective-permute-start(bf16[160,1024]{1,0:T(8,128)(2,1)} %get-tuple-element.48), channel_id=1, source_target_pairs={{0,2},{1,3},{2,4},{3,5},{4,6},{5,7},{6,0},{7,1},{8,10},{9,11},{10,... | collective-permute-start | bytes 983048 | tf_op jit(solution)/shard_map/ppermute | solution.py:360
  110.2 11.2 %collective-permute-done.31 = bf16[8,2,64,256]{3,2,1,0:T(8,128)(2,1)} collective-permute-done((bf16[8,2,64,256]{3,2,1,0:T(8,128)(2,1)}, bf16[8,2,64,256]{3,2,1,0:T(8,128)(2,1)}, u32[]{:S(2)}, u32[]{:S(2)}) %collective-permute-start.31) | collective-permute-done | bytes 524320 | tf_op jit(solution)/shard_map/ppermute | solution.py:456
  121.5 2.1 %fusion = bf16[8,2,64,256]{3,2,1,0:T(8,128)(2,1)} fusion(bf16[8,2,64,256]{3,2,1,0:T(8,128)(2,1)} %collective-permute-done.31, s32[]{:T(128)S(6)} %select_n.13, bf16[2,8,1,64,256]{4,3,2,1,0:T(8,128)(2,1)} %bitcast.26, bf16[2,8,1,64,256]{4,3,2,1,0:T(8,128)(2,1)} %bitcast.28), kind=kLoop, calls=%fused_computation.5 | loop fusion | flops 1310720 | bytes 2097156 | tf_op jit(solution)/shard_map/convert_element_type | solution.py:268
  123.6 4.1 %all-to-all-start = ((bf16[8,2,64,256]{3,2,1,0:T(8,128)(2,1)}), bf16[8,2,64,256]{3,2,1,0:T(8,128)(2,1)}, u32[]{:S(2)}, u32[]{:S(2)}) async-start(bf16[8,2,64,256]{3,2,1,0:T(8,128)(2,1)} %fusion), calls=%async_computation | async-start | bytes 1048576 | tf_op jit(solution)/shard_map/all_to_all | solution.py:457
  128.0 2.5 %collective-permute-start.19 = (bf16[144,1024]{1,0:T(8,128)(2,1)S(1)}, bf16[144,1024]{1,0:T(8,128)(2,1)S(1)}, u32[]{:S(2)}, u32[]{:S(2)}) collective-permute-start(bf16[144,1024]{1,0:T(8,128)(2,1)S(1)} %get-tuple-element.52), channel_id=1, source_target_pairs={{0,2},{1,3},{2,4},{3,5},{4,6},{5,7},{6,0},{7,1},{8,10},{9,11},{10,... | collective-permute-start | bytes 884744 | tf_op jit(solution)/shard_map/ppermute | solution.py:360
  130.5 3.2 %collective-permute-start.17 = (bf16[144,1024]{1,0:T(8,128)(2,1)S(1)}, bf16[144,1024]{1,0:T(8,128)(2,1)S(1)}, u32[]{:S(2)}, u32[]{:S(2)}) collective-permute-start(bf16[144,1024]{1,0:T(8,128)(2,1)S(1)} %get-tuple-element.50), channel_id=1, source_target_pairs={{0,2},{1,3},{2,4},{3,5},{4,6},{5,7},{6,0},{7,1},{8,10},{9,11},{10,... | collective-permute-start | bytes 884744 | tf_op jit(solution)/shard_map/ppermute | solution.py:360
  133.7 4.2 %collective-permute-done.19.got_right = bf16[144,1024]{1,0:T(8,128)(2,1)S(1)} collective-permute-done((bf16[144,1024]{1,0:T(8,128)(2,1)S(1)}, bf16[144,1024]{1,0:T(8,128)(2,1)S(1)}, u32[]{:S(2)}, u32[]{:S(2)}) %collective-permute-start.19) | collective-permute-done | bytes 294944 | tf_op jit(solution)/shard_map/ppermute | solution.py:360
  137.9 3.6 %collective-permute-done.20.got_left = bf16[144,1024]{1,0:T(8,128)(2,1)S(1)} collective-permute-done((bf16[144,1024]{1,0:T(8,128)(2,1)S(1)}, bf16[144,1024]{1,0:T(8,128)(2,1)S(1)}, u32[]{:S(2)}, u32[]{:S(2)}) %collective-permute-start.20) | collective-permute-done | bytes 294944 | tf_op jit(solution)/shard_map/ppermute | solution.py:360
  141.7 1.5 collective-permute-start.21
  143.2 2.7 %collective-permute-done.18.got_left = bf16[144,1024]{1,0:T(8,128)(2,1)S(1)} collective-permute-done((bf16[144,1024]{1,0:T(8,128)(2,1)S(1)}, bf16[144,1024]{1,0:T(8,128)(2,1)S(1)}, u32[]{:S(2)}, u32[]{:S(2)}) %collective-permute-start.18) | collective-permute-done | bytes 294944 | tf_op jit(solution)/shard_map/ppermute | solution.py:360
  145.9 4.1 %collective-permute-done.21.got_far = bf16[144,1024]{1,0:T(8,128)(2,1)S(1)} collective-permute-done((bf16[144,1024]{1,0:T(8,128)(2,1)S(1)}, bf16[144,1024]{1,0:T(8,128)(2,1)S(1)}, u32[]{:S(2)}, u32[]{:S(2)}) %collective-permute-start.21) | collective-permute-done | bytes 294944 | tf_op jit(solution)/shard_map/ppermute | solution.py:360
  150.0 3.1 %shard_map.236 = bf16[576,512]{1,0:T(8,128)(2,1)} custom-call(bf16[144,1024]{1,0:T(8,128)(2,1)S(1)} %get-tuple-element.43.coarse, bf16[576,1024]{1,0:T(8,128)(2,1)S(1)} %get-tuple-element.45.near, bf16[144,1024]{1,0:T(8,128)(2,1)S(1)} %collective-permute-done.17.got_right, bf16[144,1024]{1,0:T(8,128)(2,1)S(1)} %collective-permute-done.18.got_left, ...), custom_call_target="tpu_custom_call" | custom-call | flops 1000000000 | bytes 7735552 | tf_op jit(solution)/shard_map/pallas_call | solution.py:340
  153.1 1.1 convert_reduce_fusion
  (120 shorter events, 10.4 us)
Async XLA Ops:
  0.6 17.4 %copy-start.11 = (s32[1,576]{1,0:T(1,128)S(1)}, s32[1,576]{1,0:T(1,128)}, u32[]{:S(2)}) copy-start(s32[1,576]{1,0:T(1,128)} %constant.51.clone.n2m) | copy-start | bytes 6916
  0.6 17.4 %copy-start.2 = (bf16[2,12,24,512]{3,2,1,0:T(8,128)(2,1)S(1)}, bf16[2,12,24,512]{3,2,1,0:T(8,128)(2,1)}, u32[]{:S(2)}) copy-start(bf16[2,12,24,512]{3,2,1,0:T(8,128)(2,1)} %param.36) | copy-start | bytes 1769476
  10.1 13.4 %collective-permute-start = (bf16[288,512]{1,0:T(8,128)(2,1)S(1)}, bf16[288,512]{1,0:T(8,128)(2,1)S(1)}, u32[]{:S(2)}, u32[]{:S(2)}) collective-permute-start(bf16[288,512]{1,0:T(8,128)(2,1)S(1)} %get-tuple-element.35), channel_id=1, source_target_pairs={{0,15},{1,0},{2,1},{3,2},{4,3},{5,4},{6,5},{7,6},{8,7},{9,8},{10,9... | collective-permute-start | bytes 884744 | tf_op jit(solution)/shard_map/ppermute | solution.py:369
  10.4 13.1 %collective-permute-start.1 = (bf16[48,512]{1,0:T(8,128)(2,1)S(1)}, bf16[48,512]{1,0:T(8,128)(2,1)S(1)}, u32[]{:S(2)}, u32[]{:S(2)}) collective-permute-start(bf16[48,512]{1,0:T(8,128)(2,1)S(1)} %get-tuple-element.36), channel_id=1, source_target_pairs={{0,240},{16,0},{32,16},{48,32},{64,48},{80,64},{96,80},{112,96},{1... | collective-permute-start | bytes 147464 | tf_op jit(solution)/shard_map/ppermute | solution.py:369
  17.2 6.3 %collective-permute-start.2 = (bf16[48,512]{1,0:T(8,128)(2,1)S(1)}, bf16[48,512]{1,0:T(8,128)(2,1)S(1)}, u32[]{:S(2)}, u32[]{:S(2)}) collective-permute-start(bf16[48,512]{1,0:T(8,128)(2,1)S(1)} %get-tuple-element.37), channel_id=1, source_target_pairs={{0,255},{1,240},{2,241},{3,242},{4,243},{5,244},{6,245},{7,246},{8... | collective-permute-start | bytes 147464 | tf_op jit(solution)/shard_map/ppermute | solution.py:368
  22.9 14.6 %collective-permute-start.24 = (bf16[144,1024]{1,0:T(8,128)(2,1)S(1)}, bf16[144,1024]{1,0:T(8,128)(2,1)S(1)}, u32[]{:S(2)}, u32[]{:S(2)}) collective-permute-start(bf16[144,1024]{1,0:T(8,128)(2,1)S(1)} %shard_map.237.own), channel_id=1, source_target_pairs={{0,6},{1,7},{2,0},{3,1},{4,2},{5,3},{6,4},{7,5},{8,14},{9,15},{10,... | collective-permute-start | bytes 884744 | tf_op jit(solution)/shard_map/ppermute | solution.py:360
  24.5 13.0 %copy-start.31 = (bf16[2048]{0:T(1024)(128)(2,1)S(1)}, bf16[2048]{0:T(1024)(128)(2,1)}, u32[]{:S(2)}) copy-start(bf16[2048]{0:T(1024)(128)(2,1)} %param.30) | copy-start | bytes 12292
  24.5 13.0 %copy-start.32 = (bf16[1024]{0:T(1024)(128)(2,1)S(1)}, bf16[1024]{0:T(1024)(128)(2,1)}, u32[]{:S(2)}) copy-start(bf16[1024]{0:T(1024)(128)(2,1)} %param.32) | copy-start | bytes 6148
  24.5 17.1 %copy-start.12 = (bf16[2048,1024]{1,0:T(8,128)(2,1)S(1)}, bf16[2048,1024]{1,0:T(8,128)(2,1)}, u32[]{:S(2)}) copy-start(bf16[2048,1024]{1,0:T(8,128)(2,1)} %w_merge.1) | copy-start | bytes 12582916
  24.5 17.1 %copy-start.15 = (bf16[512,512]{1,0:T(8,128)(2,1)S(1)}, bf16[512,512]{1,0:T(8,128)(2,1)}, u32[]{:S(2)}) copy-start(bf16[512,512]{1,0:T(8,128)(2,1)} %w_proj.1) | copy-start | bytes 1572868
  24.5 17.1 %copy-start.24 = (s32[1,96]{1,0:T(1,128)S(1)}, s32[1,96]{1,0:T(1,128)}, u32[]{:S(2)}) copy-start(s32[1,96]{1,0:T(1,128)} %constant.55.clone.e2m) | copy-start | bytes 1156
  24.5 17.1 %copy-start.26 = (f32[576,512]{1,0:T(8,128)S(1)}, f32[576,512]{1,0:T(8,128)}, u32[]{:S(2)}) copy-start(f32[576,512]{1,0:T(8,128)} %copy-done.25) | copy-start | bytes 3538948
  29.7 11.9 %collective-permute-start.3 = (bf16[288,512]{1,0:T(8,128)(2,1)S(1)}, bf16[288,512]{1,0:T(8,128)(2,1)S(1)}, u32[]{:S(2)}, u32[]{:S(2)}) collective-permute-start(bf16[288,512]{1,0:T(8,128)(2,1)S(1)} %get-tuple-element.39), channel_id=1, source_target_pairs={{0,1},{1,2},{2,3},{3,4},{4,5},{5,6},{6,7},{7,8},{8,9},{9,10},{10,1... | collective-permute-start | bytes 884744 | tf_op jit(solution)/shard_map/ppermute | solution.py:369
  31.8 17.3 %collective-permute-start.22 = (bf16[144,1024]{1,0:T(8,128)(2,1)S(1)}, bf16[144,1024]{1,0:T(8,128)(2,1)S(1)}, u32[]{:S(2)}, u32[]{:S(2)}) collective-permute-start(bf16[144,1024]{1,0:T(8,128)(2,1)S(1)} %shard_map.237.own), channel_id=1, source_target_pairs={{0,8},{1,9},{2,10},{3,11},{4,12},{5,13},{6,14},{7,15},{8,0},{9,1},... | collective-permute-start | bytes 884744 | tf_op jit(solution)/shard_map/ppermute | solution.py:360
  34.4 6.4 %collective-permute-start.4 = (bf16[48,512]{1,0:T(8,128)(2,1)S(1)}, bf16[48,512]{1,0:T(8,128)(2,1)S(1)}, u32[]{:S(2)}, u32[]{:S(2)}) collective-permute-start(bf16[48,512]{1,0:T(8,128)(2,1)S(1)} %get-tuple-element.40), channel_id=1, source_target_pairs={{0,16},{16,32},{32,48},{48,64},{64,80},{80,96},{96,112},{112,128},... | collective-permute-start | bytes 147464 | tf_op jit(solution)/shard_map/ppermute | solution.py:369
  34.4 7.2 %collective-permute-start.5 = (bf16[48,512]{1,0:T(8,128)(2,1)S(1)}, bf16[48,512]{1,0:T(8,128)(2,1)S(1)}, u32[]{:S(2)}, u32[]{:S(2)}) collective-permute-start(bf16[48,512]{1,0:T(8,128)(2,1)S(1)} %get-tuple-element.41), channel_id=1, source_target_pairs={{0,17},{1,18},{2,19},{3,20},{4,21},{5,22},{6,23},{7,24},{8,25},{9,... | collective-permute-start | bytes 147464 | tf_op jit(solution)/shard_map/ppermute | solution.py:368
  37.5 11.8 %collective-permute-start.23 = (bf16[144,1024]{1,0:T(8,128)(2,1)S(1)}, bf16[144,1024]{1,0:T(8,128)(2,1)S(1)}, u32[]{:S(2)}, u32[]{:S(2)}) collective-permute-start(bf16[144,1024]{1,0:T(8,128)(2,1)S(1)} %shard_map.237.own), channel_id=1, source_target_pairs={{0,2},{1,3},{2,4},{3,5},{4,6},{5,7},{6,0},{7,1},{8,10},{9,11},{10,... | collective-permute-start | bytes 884744 | tf_op jit(solution)/shard_map/ppermute | solution.py:360
  41.6 7.7 %copy-start.16 = (bf16[1024,256]{1,0:T(8,128)(2,1)S(1)}, bf16[1024,256]{1,0:T(8,128)(2,1)}, u32[]{:S(2)}) copy-start(bf16[1024,256]{1,0:T(8,128)(2,1)} %w_in.3) | copy-start | bytes 1572868
  43.6 11.0 %copy-start.17 = (bf16[256,1024]{1,0:T(8,128)(2,1)S(1)}, bf16[256,1024]{1,0:T(8,128)(2,1)}, u32[]{:S(2)}) copy-start(bf16[256,1024]{1,0:T(8,128)(2,1)} %w_out.5) | copy-start | bytes 1572868
  43.6 11.0 %collective-permute-start.6 = (bf16[144,1024]{1,0:T(8,128)(2,1)S(1)}, bf16[144,1024]{1,0:T(8,128)(2,1)S(1)}, u32[]{:S(2)}, u32[]{:S(2)}) collective-permute-start(bf16[144,1024]{1,0:T(8,128)(2,1)S(1)} %get-tuple-element.44.own), channel_id=1, source_target_pairs={{0,8},{1,9},{2,10},{3,11},{4,12},{5,13},{6,14},{7,15},{8,0},{9,1},... | collective-permute-start | bytes 884744 | tf_op jit(solution)/shard_map/ppermute | solution.py:360
  44.2 10.4 %collective-permute-start.7 = (bf16[144,1024]{1,0:T(8,128)(2,1)S(1)}, bf16[144,1024]{1,0:T(8,128)(2,1)S(1)}, u32[]{:S(2)}, u32[]{:S(2)}) collective-permute-start(bf16[144,1024]{1,0:T(8,128)(2,1)S(1)} %get-tuple-element.44.own), channel_id=1, source_target_pairs={{0,2},{1,3},{2,4},{3,5},{4,6},{5,7},{6,0},{7,1},{8,10},{9,11},{10,... | collective-permute-start | bytes 884744 | tf_op jit(solution)/shard_map/ppermute | solution.py:360
  49.1 19.3 %collective-permute-start.26 = (bf16[208,1024]{1,0:T(8,128)(2,1)S(1)}, bf16[208,1024]{1,0:T(8,128)(2,1)S(1)}, u32[]{:S(2)}, u32[]{:S(2)}) collective-permute-start(bf16[208,1024]{1,0:T(8,128)(2,1)S(1)} %pad_maximum_fusion.3), channel_id=1, source_target_pairs={{0,6},{1,7},{2,0},{3,1},{4,2},{5,3},{6,4},{7,5},{8,14},{9,15},{10,... | collective-permute-start | bytes 1277960 | tf_op jit(solution)/shard_map/ppermute | solution.py:360
  49.2 18.0 %collective-permute-start.8 = (bf16[144,1024]{1,0:T(8,128)(2,1)S(1)}, bf16[144,1024]{1,0:T(8,128)(2,1)S(1)}, u32[]{:S(2)}, u32[]{:S(2)}) collective-permute-start(bf16[144,1024]{1,0:T(8,128)(2,1)S(1)} %get-tuple-element.44.own), channel_id=1, source_target_pairs={{0,6},{1,7},{2,0},{3,1},{4,2},{5,3},{6,4},{7,5},{8,14},{9,15},{10,... | collective-permute-start | bytes 884744 | tf_op jit(solution)/shard_map/ppermute | solution.py:360
  49.3 34.9 %collective-permute-start.9 = (bf16[1024,256]{1,0:T(8,128)(2,1)S(1)}, bf16[1024,256]{1,0:T(8,128)(2,1)S(1)}, u32[]{:S(2)}, u32[]{:S(2)}) collective-permute-start(bf16[1024,256]{1,0:T(8,128)(2,1)S(1)} %copy-done.16), channel_id=1, source_target_pairs={{0,1},{1,0},{2,3},{3,2},{4,5},{5,4},{6,7},{7,6},{8,9},{9,8},{10,11... | collective-permute-start | bytes 1572872 | tf_op jit(solution)/shard_map/ppermute | solution.py:360
  54.6 31.1 %collective-permute-start.10 = (bf16[256,1024]{1,0:T(8,128)(2,1)S(1)}, bf16[256,1024]{1,0:T(8,128)(2,1)S(1)}, u32[]{:S(2)}, u32[]{:S(2)}) collective-permute-start(bf16[256,1024]{1,0:T(8,128)(2,1)S(1)} %copy-done.17), channel_id=1, source_target_pairs={{0,1},{1,0},{2,3},{3,2},{4,5},{5,4},{6,7},{7,6},{8,9},{9,8},{10,11... | collective-permute-start | bytes 1572872 | tf_op jit(solution)/shard_map/ppermute | solution.py:360
  54.6 14.8 %collective-permute-start.25 = (bf16[224,1024]{1,0:T(8,128)(2,1)S(1)}, bf16[224,1024]{1,0:T(8,128)(2,1)S(1)}, u32[]{:S(2)}, u32[]{:S(2)}) collective-permute-start(bf16[224,1024]{1,0:T(8,128)(2,1)S(1)} %pad_maximum_fusion.1), channel_id=1, source_target_pairs={{0,2},{1,3},{2,4},{3,5},{4,6},{5,7},{6,0},{7,1},{8,10},{9,11},{10,... | collective-permute-start | bytes 1376264 | tf_op jit(solution)/shard_map/ppermute | solution.py:360
  67.2 14.8 %collective-permute-start.11 = (bf16[224,1024]{1,0:T(8,128)(2,1)S(1)}, bf16[224,1024]{1,0:T(8,128)(2,1)S(1)}, u32[]{:S(2)}, u32[]{:S(2)}) collective-permute-start(bf16[224,1024]{1,0:T(8,128)(2,1)S(1)} %pad_maximum_fusion), channel_id=1, source_target_pairs={{0,2},{1,3},{2,4},{3,5},{4,6},{5,7},{6,0},{7,1},{8,10},{9,11},{10,... | collective-permute-start | bytes 1376264 | tf_op jit(solution)/shard_map/ppermute | solution.py:360
  68.4 13.7 %collective-permute-start.12 = (bf16[208,1024]{1,0:T(8,128)(2,1)S(1)}, bf16[208,1024]{1,0:T(8,128)(2,1)S(1)}, u32[]{:S(2)}, u32[]{:S(2)}) collective-permute-start(bf16[208,1024]{1,0:T(8,128)(2,1)S(1)} %pad_maximum_fusion.2), channel_id=1, source_target_pairs={{0,6},{1,7},{2,0},{3,1},{4,2},{5,3},{6,4},{7,5},{8,14},{9,15},{10,... | collective-permute-start | bytes 1277960 | tf_op jit(solution)/shard_map/ppermute | solution.py:360
  69.4 25.0 %collective-permute-start.28 = (bf16[64,1024]{1,0:T(8,128)(2,1)S(1)}, bf16[64,1024]{1,0:T(8,128)(2,1)S(1)}, u32[]{:S(2)}, u32[]{:S(2)}) collective-permute-start(bf16[64,1024]{1,0:T(8,128)(2,1)S(1)} %slice.47), channel_id=1, source_target_pairs={{0,6},{1,7},{2,0},{3,1},{4,2},{5,3},{6,4},{7,5},{8,14},{9,15},{10,... | collective-permute-start | bytes 393224 | tf_op jit(solution)/shard_map/ppermute | solution.py:360
  82.0 12.3 %collective-permute-start.27 = (bf16[80,1024]{1,0:T(8,128)(2,1)S(1)}, bf16[80,1024]{1,0:T(8,128)(2,1)S(1)}, u32[]{:S(2)}, u32[]{:S(2)}) collective-permute-start(bf16[80,1024]{1,0:T(8,128)(2,1)S(1)} %slice.46), channel_id=1, source_target_pairs={{0,2},{1,3},{2,4},{3,5},{4,6},{5,7},{6,0},{7,1},{8,10},{9,11},{10,... | collective-permute-start | bytes 491528 | tf_op jit(solution)/shard_map/ppermute | solution.py:360
  82.1 6.3 %collective-permute-start.14 = (bf16[64,1024]{1,0:T(8,128)(2,1)S(1)}, bf16[64,1024]{1,0:T(8,128)(2,1)S(1)}, u32[]{:S(2)}, u32[]{:S(2)}) collective-permute-start(bf16[64,1024]{1,0:T(8,128)(2,1)S(1)} %slice.43), channel_id=1, source_target_pairs={{0,6},{1,7},{2,0},{3,1},{4,2},{5,3},{6,4},{7,5},{8,14},{9,15},{10,... | collective-permute-start | bytes 393224 | tf_op jit(solution)/shard_map/ppermute | solution.py:360
  84.2 5.6 %collective-permute-start.13 = (bf16[80,1024]{1,0:T(8,128)(2,1)S(1)}, bf16[80,1024]{1,0:T(8,128)(2,1)S(1)}, u32[]{:S(2)}, u32[]{:S(2)}) collective-permute-start(bf16[80,1024]{1,0:T(8,128)(2,1)S(1)} %slice.42), channel_id=1, source_target_pairs={{0,2},{1,3},{2,4},{3,5},{4,6},{5,7},{6,0},{7,1},{8,10},{9,11},{10,... | collective-permute-start | bytes 491528 | tf_op jit(solution)/shard_map/ppermute | solution.py:360
  88.1 7.0 %copy-start.8 = (bf16[144,1024]{1,0:T(8,128)(2,1)S(1)}, bf16[144,1024]{1,0:T(8,128)(2,1)}, u32[]{:S(2)}) copy-start(bf16[144,1024]{1,0:T(8,128)(2,1)} %copy-done.7) | copy-start | bytes 884740
  101.4 2.3 %collective-permute-start.29 = (bf16[1024,256]{1,0:T(8,128)(2,1)}, bf16[1024,256]{1,0:T(8,128)(2,1)}, u32[]{:S(2)}, u32[]{:S(2)}) collective-permute-start(bf16[1024,256]{1,0:T(8,128)(2,1)} %get-tuple-element.62), channel_id=1, source_target_pairs={{0,1},{1,0},{2,3},{3,2},{4,5},{5,4},{6,7},{7,6},{8,9},{9,8},{10,11... | collective-permute-start | bytes 1572872 | tf_op jit(solution)/shard_map/ppermute | solution.py:360
  101.4 3.4 %collective-permute-start.30 = (bf16[1024,256]{1,0:T(8,128)(2,1)}, bf16[1024,256]{1,0:T(8,128)(2,1)}, u32[]{:S(2)}, u32[]{:S(2)}) collective-permute-start(bf16[1024,256]{1,0:T(8,128)(2,1)} %get-tuple-element.64), channel_id=1, source_target_pairs={{0,1},{1,0},{2,3},{3,2},{4,5},{5,4},{6,7},{7,6},{8,9},{9,8},{10,11... | collective-permute-start | bytes 1572872 | tf_op jit(solution)/shard_map/ppermute | solution.py:360
  107.2 14.3 %collective-permute-start.31 = (bf16[8,2,64,256]{3,2,1,0:T(8,128)(2,1)}, bf16[8,2,64,256]{3,2,1,0:T(8,128)(2,1)}, u32[]{:S(2)}, u32[]{:S(2)}) collective-permute-start(bf16[8,2,64,256]{3,2,1,0:T(8,128)(2,1)} %fusion.2), channel_id=1, source_target_pairs={{0,128},{16,144},{32,160},{48,176},{64,192},{80,208},{96,224},{112... | collective-permute-start | bytes 1572872 | tf_op jit(solution)/shard_map/ppermute | solution.py:456
  107.8 20.0 %collective-permute-start.15 = (bf16[160,1024]{1,0:T(8,128)(2,1)}, bf16[160,1024]{1,0:T(8,128)(2,1)S(1)}, u32[]{:S(2)}, u32[]{:S(2)}) collective-permute-start(bf16[160,1024]{1,0:T(8,128)(2,1)} %get-tuple-element.48), channel_id=1, source_target_pairs={{0,2},{1,3},{2,4},{3,5},{4,6},{5,7},{6,0},{7,1},{8,10},{9,11},{10,... | collective-permute-start | bytes 983048 | tf_op jit(solution)/shard_map/ppermute | solution.py:360
  110.2 17.6 %copy-start.4 = (bf16[144,1024]{1,0:T(8,128)(2,1)S(1)}, bf16[144,1024]{1,0:T(8,128)(2,1)}, u32[]{:S(2)}) copy-start(bf16[144,1024]{1,0:T(8,128)(2,1)} %copy-done.3) | copy-start | bytes 884740
  110.2 17.6 %copy-start.6 = (bf16[144,1024]{1,0:T(8,128)(2,1)S(1)}, bf16[144,1024]{1,0:T(8,128)(2,1)}, u32[]{:S(2)}) copy-start(bf16[144,1024]{1,0:T(8,128)(2,1)} %copy-done.5) | copy-start | bytes 884740
  110.2 17.5 %collective-permute-start.16 = (bf16[128,1024]{1,0:T(8,128)(2,1)}, bf16[128,1024]{1,0:T(8,128)(2,1)S(1)}, u32[]{:S(2)}, u32[]{:S(2)}) collective-permute-start(bf16[128,1024]{1,0:T(8,128)(2,1)} %copy-done.18), channel_id=1, source_target_pairs={{0,6},{1,7},{2,0},{3,1},{4,2},{5,3},{6,4},{7,5},{8,14},{9,15},{10,... | collective-permute-start | bytes 786440 | tf_op jit(solution)/shard_map/ppermute | solution.py:360
  123.6 29.5 %all-to-all-start = ((bf16[8,2,64,256]{3,2,1,0:T(8,128)(2,1)}), bf16[8,2,64,256]{3,2,1,0:T(8,128)(2,1)}, u32[]{:S(2)}, u32[]{:S(2)}) async-start(bf16[8,2,64,256]{3,2,1,0:T(8,128)(2,1)} %fusion), calls=%async_computation | async-start | bytes 1048576 | tf_op jit(solution)/shard_map/all_to_all | solution.py:457
  127.8 22.2 %copy-start.1 = (bf16[1024,2048]{1,0:T(8,128)(2,1)S(1)}, bf16[1024,2048]{1,0:T(8,128)(2,1)}, u32[]{:S(2)}) copy-start(bf16[1024,2048]{1,0:T(8,128)(2,1)} %w_expand.3) | copy-start | bytes 12582916
  128.0 22.0 %copy-start.9 = (s32[1,576]{1,0:T(1,128)S(1)}, s32[1,576]{1,0:T(1,128)}, u32[]{:S(2)}) copy-start(s32[1,576]{1,0:T(1,128)} %constant.56.clone.m2n) | copy-start | bytes 6916
  128.0 10.0 %collective-permute-start.19 = (bf16[144,1024]{1,0:T(8,128)(2,1)S(1)}, bf16[144,1024]{1,0:T(8,128)(2,1)S(1)}, u32[]{:S(2)}, u32[]{:S(2)}) collective-permute-start(bf16[144,1024]{1,0:T(8,128)(2,1)S(1)} %get-tuple-element.52), channel_id=1, source_target_pairs={{0,2},{1,3},{2,4},{3,5},{4,6},{5,7},{6,0},{7,1},{8,10},{9,11},{10,... | collective-permute-start | bytes 884744 | tf_op jit(solution)/shard_map/ppermute | solution.py:360
  130.5 11.1 %collective-permute-start.20 = (bf16[144,1024]{1,0:T(8,128)(2,1)S(1)}, bf16[144,1024]{1,0:T(8,128)(2,1)S(1)}, u32[]{:S(2)}, u32[]{:S(2)}) collective-permute-start(bf16[144,1024]{1,0:T(8,128)(2,1)S(1)} %get-tuple-element.53), channel_id=1, source_target_pairs={{0,6},{1,7},{2,0},{3,1},{4,2},{5,3},{6,4},{7,5},{8,14},{9,15},{10,... | collective-permute-start | bytes 884744 | tf_op jit(solution)/shard_map/ppermute | solution.py:360
  130.5 12.7 %collective-permute-start.17 = (bf16[144,1024]{1,0:T(8,128)(2,1)S(1)}, bf16[144,1024]{1,0:T(8,128)(2,1)S(1)}, u32[]{:S(2)}, u32[]{:S(2)}) collective-permute-start(bf16[144,1024]{1,0:T(8,128)(2,1)S(1)} %get-tuple-element.50), channel_id=1, source_target_pairs={{0,2},{1,3},{2,4},{3,5},{4,6},{5,7},{6,0},{7,1},{8,10},{9,11},{10,... | collective-permute-start | bytes 884744 | tf_op jit(solution)/shard_map/ppermute | solution.py:360
  133.7 12.2 %collective-permute-start.18 = (bf16[144,1024]{1,0:T(8,128)(2,1)S(1)}, bf16[144,1024]{1,0:T(8,128)(2,1)S(1)}, u32[]{:S(2)}, u32[]{:S(2)}) collective-permute-start(bf16[144,1024]{1,0:T(8,128)(2,1)S(1)} %get-tuple-element.51), channel_id=1, source_target_pairs={{0,6},{1,7},{2,0},{3,1},{4,2},{5,3},{6,4},{7,5},{8,14},{9,15},{10,... | collective-permute-start | bytes 884744 | tf_op jit(solution)/shard_map/ppermute | solution.py:360
  141.7 8.3 %collective-permute-start.21 = (bf16[144,1024]{1,0:T(8,128)(2,1)S(1)}, bf16[144,1024]{1,0:T(8,128)(2,1)S(1)}, u32[]{:S(2)}, u32[]{:S(2)}) collective-permute-start(bf16[144,1024]{1,0:T(8,128)(2,1)S(1)} %shard_map.235), channel_id=1, source_target_pairs={{0,8},{1,9},{2,10},{3,11},{4,12},{5,13},{6,14},{7,15},{8,0},{9,1},... | collective-permute-start | bytes 884744 | tf_op jit(solution)/shard_map/ppermute | solution.py:360
  (18 other events, 32.1 us)
where the time goes:
time: 156 us; the launch traced here: 155 us
  waiting for transfers between devices  59.6 us (38%)
  starting transfers between devices  46.9 us (30%)
  Pallas kernels  26.4 us (17%)
  local copies, waits for them, and re-layouts  13.2 us (8%)
  other arithmetic  7.68 us (5%)
    ppermute x25, waiting for transfers between devices, on_lat(): return lax.ppermute(value, 'lat', lat_moves(dy, dx, dcore))  44.6 us
    ppermute x25, starting transfers between devices, on_lat(): return lax.ppermute(value, 'lat', lat_moves(dy, dx, dcore))  29 us
    pallas_call x10, Pallas kernels, run(): pl.pallas_call(kernel, out_shape=tuple(outs), in_specs=[pl.BlockSpec(memo...  26.4 us
    unnamed x67, local copies, waits for them, and re-layouts  11.7 us
    ppermute x1, waiting for transfers between devices, whole(): other = lax.ppermute(other, 'lon', [(o, (o + 8) % 16) for o in range(16)])  11.2 us
    ppermute x4, starting transfers between devices, shift(): return lax.ppermute(value, axes, [(s, (s + steps) % 16) for s in range(16)])  9.26 us
    convert_element_type x3, other arithmetic, added(): return (x.astype(F32) + y.astype(F32)).astype(BF16)  4.68 us
    all_to_all x1, starting transfers between devices, whole(): lax.all_to_all(added(mine, other), 'lon', 0, 0, axis_index_groups=EIGHTS,...  4.15 us
  transfers between devices with their start and end apart: 33, of which 13 were waited for; matrix products, arithmetic and copies ran while one was open for 2% of the time, Pallas kernels for 12%

commit v1 on v0

--- a/solution.py
+++ b/solution.py
@@ -109,7 +109,7 @@
     hot = ((spots == ids[0:1, :]) | (spots == ids[1:2, :])).astype(F32).astype(BF16)
     fields = mm(order, fin[...]) + mm(mm_nt(order, hot).astype(BF16), table[...].astype(BF16))
     fields_out[...] = fields
-    normed = normed_rows(fields, gain[...].astype(F32))
+    normed = normed_rows(fields, gain[...].astype(F32).reshape(1, C1))
     up = jnp.concatenate([normed[q * COARSE : q * COARSE + 72] for q in range(4)], axis=0).astype(BF16)
     lo = jnp.concatenate([normed[q * COARSE + 72 : (q + 1) * COARSE] for q in range(4)], axis=0).astype(BF16)
     up_out[...] = up
@@ -192,14 +192,22 @@
     cn_out[...] = normed_rows(coarse.astype(F32), coarse_gain[...].astype(F32)).astype(BF16)
 
 
-def cotangent_kernel(cot, w_expand, n2m, dc_out, ordered, total):
+def quarter(source, held, sems, q):
+    cols = pl.ds(pl.multiple_of(q * C1, C1), C1)
+    return pltpu.make_async_copy(source.at[:, cols], held.at[:, cols], sems.at[q])
+
+
+def cotangent_kernel(cot, n2m, w_expand, dc_out, ordered, total, held, sems):
+    for q in range(4):
+        quarter(w_expand, held, sems, q).start()
     ordered[...] = mm(picks(TOKENS, n2m[...]), cot[...]).astype(BF16)
     total[...] = jnp.zeros_like(total)
 
     def one_place(q, carry):
+        quarter(w_expand, held, sems, q).wait()
         rows = pl.ds(pl.multiple_of(q * COARSE, 16), COARSE)
         cols = pl.ds(pl.multiple_of(q * C1, C1), C1)
-        total[...] += mm_nt(ordered[rows, :], w_expand[:, cols])
+        total[...] += mm_nt(ordered[rows, :], held[:, cols])
         return carry
 
     lax.fori_loop(0, 4, one_place, 0)
@@ -247,7 +255,7 @@
 
 def wide_kernel(
     right, left, far_right2, far_left2, w_in, w_in_far, w_out, w_out_far,
-    near_right, near_left, send_right, send_left, full, hidden, slope, partial,
+    sides, send_right, send_left, full, hidden, slope, partial,
 ):
     full[0:NEAR, :] = right[0:NEAR, :]
     full[NEAR:COARSE, :] = left[0 : COARSE - NEAR, :]
@@ -256,8 +264,7 @@
     full[3 * COARSE : 3 * COARSE + NEAR, :] = far_right2[...]
     full[3 * COARSE + NEAR :, :] = far_left2[...]
     hidden_rows(full, w_in, w_in_far, w_out, w_out_far, hidden, slope, partial)
-    near_right[...] = partial[2 * COARSE : 3 * COARSE, :]
-    near_left[...] = partial[COARSE : 2 * COARSE, :]
+    sides[...] = partial[COARSE : 3 * COARSE, :]
     send_right[0:NEAR, :] = partial[0:NEAR, :]
     send_right[NEAR:, :] = partial[3 * COARSE : 3 * COARSE + NEAR, :]
     send_left[0 : COARSE - NEAR, :] = partial[NEAR:COARSE, :]
@@ -268,16 +275,17 @@
     return (x.astype(F32) + y.astype(F32)).astype(BF16)
 
 
-def pass_kernel(near, far_right, far_left, got_right, got_left, own_r, own_l, far_r, far_l):
+def pass_kernel(near, sides, got_right, got_left, own_r, own_l, far_r, far_l):
     rest = COARSE - NEAR
+    far_left, far_right = sides[0:COARSE, :], sides[COARSE:, :]
     own_r[0:NEAR, :] = added(near[3 * COARSE : 3 * COARSE + NEAR, :], got_right[0:NEAR, :])
     own_r[NEAR:, :] = near[3 * COARSE + NEAR :, :]
     own_l[0:NEAR, :] = near[2 * COARSE : 2 * COARSE + NEAR, :]
     own_l[NEAR:, :] = added(near[2 * COARSE + NEAR : 3 * COARSE, :], got_left[0:rest, :])
-    far_r[0:NEAR, :] = added(far_right[0:NEAR, :], got_right[NEAR:, :])
-    far_r[NEAR:, :] = far_right[NEAR:, :]
-    far_l[0:NEAR, :] = far_left[0:NEAR, :]
-    far_l[NEAR:, :] = added(far_left[NEAR:, :], got_left[rest:, :])
+    far_r[0:NEAR, :] = added(far_right[0:NEAR], got_right[NEAR:, :])
+    far_r[NEAR:, :] = far_right[NEAR:]
+    far_l[0:NEAR, :] = far_left[0:NEAR]
+    far_l[NEAR:, :] = added(far_left[NEAR:], got_left[rest:, :])
 
 
 def far_kernel(near, got_right, got_left, send):
@@ -286,16 +294,10 @@
 
 
 def gradient_kernel(
-    own, far, right, left, right2, left2, far_right2, far_left2, near_full, near_hidden, near_slope,
-    wide_full, wide_hidden, wide_slope, w_out, w_out_far, in_own, in_far, out_own, out_far, dfull, dact,
+    own, far, right, left, right2, left2, far_rows, near_full, near_hidden, near_slope,
+    wide_full, wide_hidden, wide_slope, w_out, w_out_far, own_sums, far_sums, dfull, dact,
 ):
-    stack_into(dfull, (own, far, right, left))
-    dfull[QUAD : QUAD + NEAR, :] = right2[0:NEAR, :]
-    dfull[QUAD + NEAR : QUAD + COARSE, :] = left2[0 : COARSE - NEAR, :]
-    dfull[QUAD + COARSE : QUAD + 2 * COARSE, :] = right2[NEAR:, :]
-    dfull[QUAD + 2 * COARSE : QUAD + 3 * COARSE, :] = left2[COARSE - NEAR :, :]
-    dfull[QUAD + 3 * COARSE : QUAD + 3 * COARSE + NEAR, :] = far_right2[...]
-    dfull[QUAD + 3 * COARSE + NEAR :, :] = far_left2[...]
+    stack_into(dfull, (own, far, right, left, right2, left2, far_rows))
     for side, wout in enumerate((w_out, w_out_far)):
         cols = slice(side * FB, (side + 1) * FB)
         for part, slope in enumerate((near_slope, wide_slope)):
@@ -305,18 +307,28 @@
 
     def one_block(k, carry):
         c = pl.ds(pl.multiple_of(k * 256, 256), 256)
-        both = mm_tn(dfull[0:QUAD, c], near_hidden[...]) + mm_tn(dfull[QUAD:, c], wide_hidden[...])
-        out_own[c, :] = both[:, :FB].astype(BF16)
-        out_far[c, :] = both[:, FB:].astype(BF16)
-        both = mm_tn(near_full[:, c], dact[0:QUAD, :]) + mm_tn(wide_full[:, c], dact[QUAD:, :])
-        in_own[c, :] = both[:, :FB].astype(BF16)
-        in_far[c, :] = both[:, FB:].astype(BF16)
+        out = mm_tn(dfull[0:QUAD, c], near_hidden[...]) + mm_tn(dfull[QUAD:, c], wide_hidden[...])
+        into = mm_tn(near_full[:, c], dact[0:QUAD, :]) + mm_tn(wide_full[:, c], dact[QUAD:, :])
+        for g, both in enumerate((out, into)):
+            both = both.astype(BF16)
+            for i in range(4):
+                rows = pl.ds(pl.multiple_of(k * 512 + i * 128 + g * 64, 64), 64)
+                own_sums[rows, :] = both[i * 64 : (i + 1) * 64, :FB]
+                far_sums[rows, :] = both[i * 64 : (i + 1) * 64, FB:]
         return carry
 
     lax.fori_loop(0, 4, one_block, 0)
 
 
-def expand_kernel(coarse, near, got_right, got_left, got_far, w_expand, skip, m2n, fields_out, parts):
+def pair_kernel(side, own, got, mine, other):
+    for out, half in ((mine, side[0]), (other, 1 - side[0])):
+        rows = pl.ds(pl.multiple_of(half * C2, C2), C2)
+        out[...] = added(own[rows, :], got[rows, :])
+
+
+def expand_kernel(coarse, near, got_right, got_left, got_far, skip, m2n, w_expand, fields_out, parts, held, sems):
+    for q in range(4):
+        quarter(w_expand, held, sems, q).start()
     mixed = near[0:COARSE, :].astype(F32) + got_right[...].astype(F32)
     mixed = mixed + (got_left[...].astype(F32) + got_far[...].astype(F32))
     coarse_out = (coarse[...].astype(F32) + mixed).astype(BF16)
@@ -324,7 +336,8 @@
     def one_place(q, carry):
         rows = pl.ds(pl.multiple_of(q * COARSE, 16), COARSE)
         cols = pl.ds(pl.multiple_of(q * C1, C1), C1)
-        parts[rows, :] = (skip[rows, :].astype(F32) + mm(coarse_out, w_expand[:, cols])).astype(BF16)
+        quarter(w_expand, held, sems, q).wait()
+        parts[rows, :] = (skip[rows, :].astype(F32) + mm(coarse_out, held[:, cols])).astype(BF16)
         return carry
 
     lax.fori_loop(0, 4, one_place, 0)
@@ -335,15 +348,19 @@
     return jax.ShapeDtypeStruct(dims, dtype)
 
 
-def run(kernel, outs, args, flops, scratch=(), smem=()):
+FETCH = (pltpu.VMEM((C2, 4 * C1), BF16), pltpu.SemaphoreType.DMA((4,)))
+
+
+def run(kernel, outs, args, flops, scratch=(), smem=(), hbm=(), vmem=20):
     nbytes = sum(a.size * a.dtype.itemsize for a in args) + sum(math.prod(o.shape) * 2 for o in outs)
+    spaces = [pltpu.SMEM if k in smem else pl.ANY if k in hbm else pltpu.VMEM for k in range(len(args))]
     return pl.pallas_call(
         kernel,
         out_shape=tuple(outs),
-        in_specs=[pl.BlockSpec(memory_space=pltpu.SMEM if k in smem else pltpu.VMEM) for k in range(len(args))],
+        in_specs=[pl.BlockSpec(memory_space=space) for space in spaces],
         out_specs=tuple(pl.BlockSpec(memory_space=pltpu.VMEM) for _ in outs),
         scratch_shapes=list(scratch),
-        compiler_params=pltpu.CompilerParams(vmem_limit_bytes=32 * 1024 * 1024),
+        compiler_params=pltpu.CompilerParams(vmem_limit_bytes=vmem and vmem * 1024 * 1024),
         cost_estimate=pl.CostEstimate(flops=int(flops), bytes_accessed=int(nbytes), transcendentals=0),
     )(*args)
 
@@ -376,6 +393,14 @@
     left2 = on_lat(jnp.concatenate([left[NEAR:], far], axis=0), dx=-1)
     far_right2, far_left2 = on_lat(right2[NEAR : 2 * NEAR], dx=1), on_lat(left2[COARSE:], dx=-1)
     return (block, far, right, left), (right2, left2, far_right2, far_left2)
+
+
+def gathered_behind(block):
+    far = on_lat(block, dy=1)
+    right, left = on_lat(block, dx=1), on_lat(block, dx=-1)
+    right2, left2 = on_lat(right[:NEAR], dx=1), on_lat(left[NEAR:], dx=-1)
+    far_rows = on_lat(jnp.concatenate([right, left, right2, left2], axis=0), dy=1)
+    return block, far, right, left, right2, left2, far_rows
 
 
 EIGHTS = [[half * 8 + z for z in range(8)] for half in range(2)]
@@ -394,17 +419,18 @@
         [shaped((TOKENS, C1), F32), shaped((HALF, C1)), shaped((HALF, C1)), shaped((EDGE, C1)), shaped((EDGE, C1))],
         (
             fields_in.reshape(TOKENS, C1), ids,
-            level_table, surface_table, norm_gain.reshape(1, C1), lanes(N2M), lanes(H2E),
+            level_table, surface_table, norm_gain, lanes(N2M), lanes(H2E),
         ),
         4e8,
         [pltpu.VMEM((16, C1), F32)],
+        vmem=None,
     )
     up, lon, diag = shift(up, "lat", -1), shift(lon, "lon", -1), shift(diag, "both", -1)
     (dc,) = run(
-        cotangent_kernel, [shaped((COARSE, C2))], (cotangent.reshape(TOKENS, C1), w_expand, lanes(N2M)), 1e9,
-        [pltpu.VMEM((TOKENS, C1), BF16), pltpu.VMEM((COARSE, C2), F32)],
-    )
-    dc_near, dc_wide = gathered(dc)
+        cotangent_kernel, [shaped((COARSE, C2))], (cotangent.reshape(TOKENS, C1), lanes(N2M), w_expand), 1e9,
+        [pltpu.VMEM((TOKENS, C1), BF16), pltpu.VMEM((COARSE, C2), F32), *FETCH], hbm=(2,), vmem=None,
+    )
+    dc_pieces = gathered_behind(dc)
     flag = (lat == 15).astype(jnp.int32).reshape(1)
     lo, up, lon, diag = run(
         attention_kernel,
@@ -425,44 +451,43 @@
     weights = (w_in, w_in_far, w_out, w_out_far)
     kept = [shaped((QUAD, C2)), shaped((QUAD, 2 * FB)), shaped((QUAD, 2 * FB))]
     near, *near_kept = run(near_kernel, [shaped((QUAD, C2)), *kept], (*cn_near, *weights), 2.5e9)
-    far_right, far_left, to_right, to_left, *wide_kept = run(
+    sides, to_right, to_left, *wide_kept = run(
         wide_kernel,
-        [shaped((COARSE, C2)), shaped((COARSE, C2)), shaped((2 * NEAR, C2)), shaped((2 * (COARSE - NEAR), C2)), *kept],
+        [shaped((2 * COARSE, C2)), shaped((2 * NEAR, C2)), shaped((2 * (COARSE - NEAR), C2)), *kept],
         (*cn_wide, *weights),
         2.5e9,
         [pltpu.VMEM((QUAD, C2), BF16)],
     )
     got_right, got_left = on_lat(to_right, dx=1), on_lat(to_left, dx=-1)
-    in_own, in_far, out_own, out_far = run(
+    own_sums, far_sums = run(
         gradient_kernel,
-        [shaped((C2, FB))] * 4,
-        (*dc_near, *dc_wide, *near_kept, *wide_kept, w_out, w_out_far),
+        [shaped((2 * C2, FB))] * 2,
+        (*dc_pieces, *near_kept, *wide_kept, w_out, w_out_far),
         4e9,
         [pltpu.VMEM((8 * COARSE, C2), BF16), pltpu.VMEM((8 * COARSE, 2 * FB), BF16)],
     )
-    own_r, own_l, far_r, far_l = run(
-        pass_kernel, [shaped((COARSE, C2))] * 4, (near, far_right, far_left, got_right, got_left), 1e8
-    )
+    own_r, own_l, far_r, far_l = run(pass_kernel, [shaped((COARSE, C2))] * 4, (near, sides, got_right, got_left), 1e8)
     far_r, far_l = on_lat(far_r, dx=1), on_lat(far_l, dx=-1)
     own_r, own_l = on_lat(own_r, dx=1), on_lat(own_l, dx=-1)
     (across,) = run(far_kernel, [shaped((COARSE, C2))], (near, far_r, far_l), 1e8)
     across = on_lat(across, dy=1)
 
-    out_sum, in_sum = added(out_own, on_lat(out_far, dcore=1)), added(in_own, on_lat(in_far, dcore=1))
-    both = jnp.stack([out_sum.reshape(2, 8, 64, FB), in_sum.reshape(2, 8, 64, FB)], axis=2)
-    side = lon_index // 8
-    mine = lax.dynamic_index_in_dim(both, side, 0, keepdims=False)
-    other = lax.dynamic_index_in_dim(both, 1 - side, 0, keepdims=False)
+    got_sums = on_lat(far_sums, dcore=1)
+    side = (lon_index // 8).astype(jnp.int32).reshape(1)
+    mine, other = run(pair_kernel, [shaped((C2, FB))] * 2, (side, own_sums, got_sums), 1e8, smem=(0,))
     other = lax.ppermute(other, "lon", [(o, (o + 8) % 16) for o in range(16)])
-    pieces = lax.all_to_all(added(mine, other), "lon", 0, 0, axis_index_groups=EIGHTS, tiled=True)
+    both = added(mine, other).reshape(8, 128, FB)
+    pieces = lax.all_to_all(both, "lon", 0, 0, axis_index_groups=EIGHTS, tiled=True)
     total = jnp.sum(pieces.astype(F32), axis=0)
-    grad_out, grad_in = total[0].T, total[1]
+    grad_out, grad_in = total[:64].T, total[64:]
     (fields_out,) = run(
         expand_kernel,
         [shaped((TOKENS, C1))],
-        (coarse, near, own_r, own_l, across, w_expand, skip, lanes(M2N)),
+        (coarse, near, own_r, own_l, across, skip, lanes(M2N), w_expand),
         1e9,
-        [pltpu.VMEM((TOKENS, C1), BF16)],
+        [pltpu.VMEM((TOKENS, C1), BF16), *FETCH],
+        hbm=(7,),
+        vmem=None,
     )
     return (fields_out.reshape(LEVELS, ROWS, COLS, C1), grad_in, grad_out)
 

time: 156 us -> 149 us (0.955)
  the two profiles are of different devices: /device:TPU:6 before, /device:TPU:54 now
where the time goes in v1:
time: 149 us; the launch traced here: 148 us
  waiting for transfers between devices  55.7 us (37%)
  starting transfers between devices  46.4 us (31%)
  Pallas kernels  33.9 us (23%)
  local copies, waits for them, and re-layouts  9.63 us (6%)
  other arithmetic  1.83 us (1%)
    ppermute x23, waiting for transfers between devices, on_lat(): return lax.ppermute(value, 'lat', lat_moves(dy, dx, dcore))  43.9 us
    pallas_call x11, Pallas kernels, run(): pl.pallas_call(kernel, out_shape=tuple(outs), in_specs=[pl.BlockSpec(memo...  33.9 us
    ppermute x23, starting transfers between devices, on_lat(): return lax.ppermute(value, 'lat', lat_moves(dy, dx, dcore))  25 us
    ppermute x1, waiting for transfers between devices, whole(): other = lax.ppermute(other, 'lon', [(o, (o + 8) % 16) for o in range(16)])  9.76 us
    unnamed x43, local copies, waits for them, and re-layouts  8.21 us
    all_to_all x1, starting transfers between devices, whole(): lax.all_to_all(both, 'lon', 0, 0, axis_index_groups=EIGHTS, tiled=True)  8.1 us
    ppermute x2, starting transfers between devices, shift(): return lax.ppermute(value, ('lon', 'lat'), pairs)  8.09 us
    ppermute x4, starting transfers between devices, shift(): return lax.ppermute(value, axes, [(s, (s + steps) % 16) for s in range(16)])  3.85 us
  transfers between devices with their start and end apart: 31, of which 15 were waited for; matrix products, arithmetic and copies ran while one was open for 1% of the time, Pallas kernels for 13%

profile of v1, /device:TPU:54, one launch (start us, length us, event | category | flops | bytes accessed | tf_op | source)
XLA Modules:
  0.0 148.4 jit_solution(17474265921399450565)
XLA Ops:
  0.6 0.7 convert_add_fusion
  1.3 0.7 copy.25
  2.1 0.7 reshape.42.ids
  2.7 3.4 %shard_map.229 = (f32[576,512]{1,0:T(8,128)}, bf16[288,512]{1,0:T(8,128)(2,1)}, bf16[288,512]{1,0:T(8,128)(2,1)}, bf16[48,512]{1,0:T(8,128)(2,1)}, bf16[48,512]{1,0:T(8,128)(2,1)}) custom-call(bf16[576,512]{1,0:T(8,128)(2,1)} %bitcast.10, s32[2,576]{1,0:T(2,128)} %reshape.42.ids, bf16[13,512]{1,0:T(8,128)(2,1)} %level_table.1, bf16[2,512]{1,0:T(2,128)(2,1)} %surface_table.1, ...), custom_call_target="tpu_custom_call" | custom-call | flops 400000000 | bytes 1892224 | tf_op jit(solution)/shard_map/pallas_call | solution.py:357
  6.5 6.4 %collective-permute-start.2 = (bf16[48,512]{1,0:T(8,128)(2,1)}, bf16[48,512]{1,0:T(8,128)(2,1)S(1)}, u32[]{:S(2)}, u32[]{:S(2)}) collective-permute-start(bf16[48,512]{1,0:T(8,128)(2,1)} %get-tuple-element.36), channel_id=1, source_target_pairs={{0,255},{1,240},{2,241},{3,242},{4,243},{5,244},{6,245},{7,246},{8... | collective-permute-start | bytes 147464 | tf_op jit(solution)/shard_map/ppermute | solution.py:385
  12.9 2.1 %collective-permute-done.2.diag = bf16[48,512]{1,0:T(8,128)(2,1)S(1)} collective-permute-done((bf16[48,512]{1,0:T(8,128)(2,1)}, bf16[48,512]{1,0:T(8,128)(2,1)S(1)}, u32[]{:S(2)}, u32[]{:S(2)}) %collective-permute-start.2) | collective-permute-done | bytes 49184 | tf_op jit(solution)/shard_map/ppermute | solution.py:385
  15.0 1.4 copy-done.7
  16.4 0.7 copy-done.11
  17.1 0.7 copy-done.12
  17.8 1.0 copy-done.15
  18.7 5.1 %shard_map.230 = (bf16[288,512]{1,0:T(8,128)(2,1)S(1)}, bf16[288,512]{1,0:T(8,128)(2,1)S(1)}, bf16[48,512]{1,0:T(8,128)(2,1)S(1)}, bf16[48,512]{1,0:T(8,128)(2,1)S(1)}) custom-call(s32[1]{0:T(128)} %bitcast.flag, bf16[288,512]{1,0:T(8,128)(2,1)S(1)} %copy-done.15, bf16[288,512]{1,0:T(8,128)(2,1)S(1)} %collective-permute-done.up, ...), custom_call_target="tpu_custom_call" | custom-call | flops 3000000000 | bytes 2954116 | tf_op jit(solution)/shard_map/pallas_call | solution.py:357
  23.9 1.6 %collective-permute-start.3 = (bf16[288,512]{1,0:T(8,128)(2,1)S(1)}, bf16[288,512]{1,0:T(8,128)(2,1)S(1)}, u32[]{:S(2)}, u32[]{:S(2)}) collective-permute-start(bf16[288,512]{1,0:T(8,128)(2,1)S(1)} %get-tuple-element.38), channel_id=1, source_target_pairs={{0,1},{1,2},{2,3},{3,4},{4,5},{5,6},{6,7},{7,8},{8,9},{9,10},{10,1... | collective-permute-start | bytes 884744 | tf_op jit(solution)/shard_map/ppermute | solution.py:386
  25.4 1.9 %collective-permute-start.4 = (bf16[48,512]{1,0:T(8,128)(2,1)S(1)}, bf16[48,512]{1,0:T(8,128)(2,1)S(1)}, u32[]{:S(2)}, u32[]{:S(2)}) collective-permute-start(bf16[48,512]{1,0:T(8,128)(2,1)S(1)} %get-tuple-element.39), channel_id=1, source_target_pairs={{0,16},{16,32},{32,48},{48,64},{64,80},{80,96},{96,112},{112,128},... | collective-permute-start | bytes 147464 | tf_op jit(solution)/shard_map/ppermute | solution.py:386
  27.3 1.7 %collective-permute-start.5 = (bf16[48,512]{1,0:T(8,128)(2,1)S(1)}, bf16[48,512]{1,0:T(8,128)(2,1)S(1)}, u32[]{:S(2)}, u32[]{:S(2)}) collective-permute-start(bf16[48,512]{1,0:T(8,128)(2,1)S(1)} %get-tuple-element.40), channel_id=1, source_target_pairs={{0,17},{1,18},{2,19},{3,20},{4,21},{5,22},{6,23},{7,24},{8,25},{9,... | collective-permute-start | bytes 147464 | tf_op jit(solution)/shard_map/ppermute | solution.py:385
  29.0 5.2 %shard_map.237.own = bf16[144,1024]{1,0:T(8,128)(2,1)} custom-call(bf16[576,512]{1,0:T(8,128)(2,1)} %bitcast.8, s32[1,576]{1,0:T(1,128)} %constant.42.clone.n2m, bf16[1024,2048]{1,0:T(8,128)(2,1)} %w_expand.3), custom_call_target="tpu_custom_call" | custom-call | flops 1000000000 | bytes 5081344 | tf_op jit(solution)/shard_map/pallas_call | solution.py:357
  34.3 2.0 %collective-permute-start.24 = (bf16[144,1024]{1,0:T(8,128)(2,1)}, bf16[144,1024]{1,0:T(8,128)(2,1)S(1)}, u32[]{:S(2)}, u32[]{:S(2)}) collective-permute-start(bf16[144,1024]{1,0:T(8,128)(2,1)} %shard_map.237.own), channel_id=1, source_target_pairs={{0,6},{1,7},{2,0},{3,1},{4,2},{5,3},{6,4},{7,5},{8,14},{9,15},{10,... | collective-permute-start | bytes 884744 | tf_op jit(solution)/shard_map/ppermute | solution.py:377
  36.4 2.2 %copy-done.6 = bf16[2048,1024]{1,0:T(8,128)(2,1)S(1)} copy-done((bf16[2048,1024]{1,0:T(8,128)(2,1)S(1)}, bf16[2048,1024]{1,0:T(8,128)(2,1)}, u32[]{:S(2)}) %copy-start.6) | copy-done | bytes 4194328
  38.6 1.9 %shard_map.231 = (bf16[576,512]{1,0:T(8,128)(2,1)S(1)}, bf16[144,1024]{1,0:T(8,128)(2,1)S(1)}, bf16[144,1024]{1,0:T(8,128)(2,1)S(1)}) custom-call(bf16[288,512]{1,0:T(8,128)(2,1)S(1)} %get-tuple-element.37.lo, bf16[288,512]{1,0:T(8,128)(2,1)S(1)} %collective-permute-done.3.up, bf16[48,512]{1,0:T(8,128)(2,1)S(1)} %collective-permute-done.4.lon, ...), custom_call_target="tpu_custom_call" | custom-call | flops 2000000000 | bytes 7772544 | tf_op jit(solution)/shard_map/pallas_call | solution.py:357
  40.5 1.6 %collective-permute-start.7 = (bf16[144,1024]{1,0:T(8,128)(2,1)S(1)}, bf16[144,1024]{1,0:T(8,128)(2,1)S(1)}, u32[]{:S(2)}, u32[]{:S(2)}) collective-permute-start(bf16[144,1024]{1,0:T(8,128)(2,1)S(1)} %get-tuple-element.43.own), channel_id=1, source_target_pairs={{0,2},{1,3},{2,4},{3,5},{4,6},{5,7},{6,0},{7,1},{8,10},{9,11},{10,... | collective-permute-start | bytes 884744 | tf_op jit(solution)/shard_map/ppermute | solution.py:377
  42.1 1.7 %collective-permute-start.6 = (bf16[144,1024]{1,0:T(8,128)(2,1)S(1)}, bf16[144,1024]{1,0:T(8,128)(2,1)S(1)}, u32[]{:S(2)}, u32[]{:S(2)}) collective-permute-start(bf16[144,1024]{1,0:T(8,128)(2,1)S(1)} %get-tuple-element.43.own), channel_id=1, source_target_pairs={{0,8},{1,9},{2,10},{3,11},{4,12},{5,13},{6,14},{7,15},{8,0},{9,1},... | collective-permute-start | bytes 884744 | tf_op jit(solution)/shard_map/ppermute | solution.py:377
  44.2 0.9 collective-permute-done.24.left
  45.2 4.8 %collective-permute-done.7.right = bf16[144,1024]{1,0:T(8,128)(2,1)S(1)} collective-permute-done((bf16[144,1024]{1,0:T(8,128)(2,1)S(1)}, bf16[144,1024]{1,0:T(8,128)(2,1)S(1)}, u32[]{:S(2)}, u32[]{:S(2)}) %collective-permute-start.7) | collective-permute-done | bytes 294944 | tf_op jit(solution)/shard_map/ppermute | solution.py:377
  50.0 2.2 %collective-permute-start.25 = (bf16[80,1024]{1,0:T(8,128)(2,1)S(1)}, bf16[80,1024]{1,0:T(8,128)(2,1)S(1)}, u32[]{:S(2)}, u32[]{:S(2)}) collective-permute-start(bf16[80,1024]{1,0:T(8,128)(2,1)S(1)} %slice.36), channel_id=1, source_target_pairs={{0,2},{1,3},{2,4},{3,5},{4,6},{5,7},{6,0},{7,1},{8,10},{9,11},{10,... | collective-permute-start | bytes 491528 | tf_op jit(solution)/shard_map/ppermute | solution.py:377
  52.7 2.9 %collective-permute-start.11 = (bf16[224,1024]{1,0:T(8,128)(2,1)S(1)}, bf16[224,1024]{1,0:T(8,128)(2,1)S(1)}, u32[]{:S(2)}, u32[]{:S(2)}) collective-permute-start(bf16[224,1024]{1,0:T(8,128)(2,1)S(1)} %pad_maximum_fusion.1), channel_id=1, source_target_pairs={{0,2},{1,3},{2,4},{3,5},{4,6},{5,7},{6,0},{7,1},{8,10},{9,11},{10,... | collective-permute-start | bytes 1376264 | tf_op jit(solution)/shard_map/ppermute | solution.py:377
  55.7 2.8 %collective-permute-done.26.left2 = bf16[64,1024]{1,0:T(8,128)(2,1)S(1)} collective-permute-done((bf16[64,1024]{1,0:T(8,128)(2,1)S(1)}, bf16[64,1024]{1,0:T(8,128)(2,1)S(1)}, u32[]{:S(2)}, u32[]{:S(2)}) %collective-permute-start.26) | collective-permute-done | bytes 131104 | tf_op jit(solution)/shard_map/ppermute | solution.py:377
  58.5 0.6 collective-permute-start.27
  59.1 9.9 %collective-permute-done.12.left = bf16[208,1024]{1,0:T(8,128)(2,1)S(1)} collective-permute-done((bf16[208,1024]{1,0:T(8,128)(2,1)S(1)}, bf16[208,1024]{1,0:T(8,128)(2,1)S(1)}, u32[]{:S(2)}, u32[]{:S(2)}) %collective-permute-start.12) | collective-permute-done | bytes 426016 | tf_op jit(solution)/shard_map/ppermute | solution.py:377
  69.4 3.5 %collective-permute-start.13 = (bf16[80,1024]{1,0:T(8,128)(2,1)S(1)}, bf16[80,1024]{1,0:T(8,128)(2,1)S(1)}, u32[]{:S(2)}, u32[]{:S(2)}) collective-permute-start(bf16[80,1024]{1,0:T(8,128)(2,1)S(1)} %slice.34), channel_id=1, source_target_pairs={{0,2},{1,3},{2,4},{3,5},{4,6},{5,7},{6,0},{7,1},{8,10},{9,11},{10,... | collective-permute-start | bytes 491528 | tf_op jit(solution)/shard_map/ppermute | solution.py:377
  72.9 2.4 %shard_map.232 = (bf16[576,1024]{1,0:T(8,128)(2,1)S(1)}, bf16[576,1024]{1,0:T(8,128)(2,1)S(1)}, bf16[576,512]{1,0:T(8,128)(2,1)S(1)}, bf16[576,512]{1,0:T(8,128)(2,1)S(1)}) custom-call(bf16[144,1024]{1,0:T(8,128)(2,1)S(1)} %get-tuple-element.43.own, bf16[144,1024]{1,0:T(8,128)(2,1)S(1)} %collective-permute-done.6.far, ...), custom_call_target="tpu_custom_call" | custom-call | flops 2500000000 | bytes 6815744 | tf_op jit(solution)/shard_map/pallas_call | solution.py:357
  75.8 3.1 %shard_map.233 = (bf16[288,1024]{1,0:T(8,128)(2,1)S(1)}, bf16[160,1024]{1,0:T(8,128)(2,1)}, bf16[128,1024]{1,0:T(8,128)(2,1)S(1)}, bf16[576,1024]{1,0:T(8,128)(2...) custom-call(bf16[224,1024]{1,0:T(8,128)(2,1)S(1)} %collective-permute-done.11.right, ...), custom_call_target="tpu_custom_call" | custom-call | flops 2500000000 | bytes 6815744 | tf_op jit(solution)/shard_map/pallas_call | solution.py:357
  78.9 0.8 copy-done.2
  79.7 5.9 %collective-permute-done.22.far = bf16[144,1024]{1,0:T(8,128)(2,1)S(1)} collective-permute-done((bf16[144,1024]{1,0:T(8,128)(2,1)S(1)}, bf16[144,1024]{1,0:T(8,128)(2,1)S(1)}, u32[]{:S(2)}, u32[]{:S(2)}) %collective-permute-start.22) | collective-permute-done | bytes 294944 | tf_op jit(solution)/shard_map/ppermute | solution.py:377
  85.7 6.5 %shard_map.238 = (bf16[2048,256]{1,0:T(8,128)(2,1)S(1)}, bf16[2048,256]{1,0:T(8,128)(2,1)}) custom-call(bf16[144,1024]{1,0:T(8,128)(2,1)S(1)} %copy-done.5, bf16[144,1024]{1,0:T(8,128)(2,1)S(1)} %collective-permute-done.22.far, bf16[144,1024]{1,0:T(8,128)(2,1)S(1)} %collective-permute-done.23.right, bf16[144,1024]{1,0:T(8,128)(2,1)S(1)} %collective-permute-done.24.left, ...), custom_call_target="tpu_custom_call" | custom-call | flops 4000000000 | bytes 10223616 | tf_op jit(solution)/shard_map/pallas_call | solution.py:357
  92.2 2.9 %collective-permute-done.28.got = bf16[2048,256]{1,0:T(8,128)(2,1)S(1)} collective-permute-done((bf16[2048,256]{1,0:T(8,128)(2,1)}, bf16[2048,256]{1,0:T(8,128)(2,1)S(1)}, u32[]{:S(2)}, u32[]{:S(2)}) %collective-permute-start.28) | collective-permute-done | bytes 1048608 | tf_op jit(solution)/shard_map/ppermute | solution.py:377
  95.3 1.3 collective-permute-start.29
  96.6 3.0 %collective-permute-start.15 = (bf16[160,1024]{1,0:T(8,128)(2,1)}, bf16[160,1024]{1,0:T(8,128)(2,1)S(1)}, u32[]{:S(2)}, u32[]{:S(2)}) collective-permute-start(bf16[160,1024]{1,0:T(8,128)(2,1)} %get-tuple-element.46), channel_id=1, source_target_pairs={{0,2},{1,3},{2,4},{3,5},{4,6},{5,7},{6,0},{7,1},{8,10},{9,11},{10,... | collective-permute-start | bytes 983048 | tf_op jit(solution)/shard_map/ppermute | solution.py:377
  99.6 9.8 %collective-permute-done.29 = bf16[1024,256]{1,0:T(8,128)(2,1)S(1)} collective-permute-done((bf16[1024,256]{1,0:T(8,128)(2,1)S(1)}, bf16[1024,256]{1,0:T(8,128)(2,1)S(1)}, u32[]{:S(2)}, u32[]{:S(2)}) %collective-permute-start.29) | collective-permute-done | bytes 524320 | tf_op jit(solution)/shard_map/ppermute | solution.py:478
  109.3 0.9 add_convert_fusion
  110.3 8.1 %all-to-all-start = ((bf16[8,128,256]{2,1,0:T(8,128)(2,1)}), bf16[8,128,256]{2,1,0:T(8,128)(2,1)S(1)}, u32[]{:S(2)}, u32[]{:S(2)}) async-start(bf16[8,128,256]{2,1,0:T(8,128)(2,1)} %bitcast.5), calls=%async_computation | async-start | bytes 1048576 | tf_op jit(solution)/shard_map/all_to_all | solution.py:480
  118.5 3.0 %collective-permute-start.19 = (bf16[144,1024]{1,0:T(8,128)(2,1)S(1)}, bf16[144,1024]{1,0:T(8,128)(2,1)S(1)}, u32[]{:S(2)}, u32[]{:S(2)}) collective-permute-start(bf16[144,1024]{1,0:T(8,128)(2,1)S(1)} %get-tuple-element.50), channel_id=1, source_target_pairs={{0,2},{1,3},{2,4},{3,5},{4,6},{5,7},{6,0},{7,1},{8,10},{9,11},{10,... | collective-permute-start | bytes 884744 | tf_op jit(solution)/shard_map/ppermute | solution.py:377
  121.6 3.2 %collective-permute-start.17 = (bf16[144,1024]{1,0:T(8,128)(2,1)S(1)}, bf16[144,1024]{1,0:T(8,128)(2,1)S(1)}, u32[]{:S(2)}, u32[]{:S(2)}) collective-permute-start(bf16[144,1024]{1,0:T(8,128)(2,1)S(1)} %get-tuple-element.48), channel_id=1, source_target_pairs={{0,2},{1,3},{2,4},{3,5},{4,6},{5,7},{6,0},{7,1},{8,10},{9,11},{10,... | collective-permute-start | bytes 884744 | tf_op jit(solution)/shard_map/ppermute | solution.py:377
  124.8 4.2 %collective-permute-done.19.got_right = bf16[144,1024]{1,0:T(8,128)(2,1)S(1)} collective-permute-done((bf16[144,1024]{1,0:T(8,128)(2,1)S(1)}, bf16[144,1024]{1,0:T(8,128)(2,1)S(1)}, u32[]{:S(2)}, u32[]{:S(2)}) %collective-permute-start.19) | collective-permute-done | bytes 294944 | tf_op jit(solution)/shard_map/ppermute | solution.py:377
  129.0 3.7 %collective-permute-done.20.got_left = bf16[144,1024]{1,0:T(8,128)(2,1)S(1)} collective-permute-done((bf16[144,1024]{1,0:T(8,128)(2,1)S(1)}, bf16[144,1024]{1,0:T(8,128)(2,1)S(1)}, u32[]{:S(2)}, u32[]{:S(2)}) %collective-permute-start.20) | collective-permute-done | bytes 294944 | tf_op jit(solution)/shard_map/ppermute | solution.py:377
  133.2 3.3 %collective-permute-done.18.got_left = bf16[144,1024]{1,0:T(8,128)(2,1)S(1)} collective-permute-done((bf16[144,1024]{1,0:T(8,128)(2,1)S(1)}, bf16[144,1024]{1,0:T(8,128)(2,1)S(1)}, u32[]{:S(2)}, u32[]{:S(2)}) %collective-permute-start.18) | collective-permute-done | bytes 294944 | tf_op jit(solution)/shard_map/ppermute | solution.py:377
  136.5 4.6 %collective-permute-done.21.got_far = bf16[144,1024]{1,0:T(8,128)(2,1)S(1)} collective-permute-done((bf16[144,1024]{1,0:T(8,128)(2,1)S(1)}, bf16[144,1024]{1,0:T(8,128)(2,1)S(1)}, u32[]{:S(2)}, u32[]{:S(2)}) %collective-permute-start.21) | collective-permute-done | bytes 294944 | tf_op jit(solution)/shard_map/ppermute | solution.py:377
  141.1 0.7 copy-done.18
  141.8 5.8 %shard_map.236 = bf16[576,512]{1,0:T(8,128)(2,1)} custom-call(bf16[144,1024]{1,0:T(8,128)(2,1)} %copy-done.4, bf16[576,1024]{1,0:T(8,128)(2,1)} %copy-done, bf16[144,1024]{1,0:T(8,128)(2,1)} %copy-done.16, bf16[144,1024]{1,0:T(8,128)(2,1)} %copy-done.17, bf16[144,1024]{1,0:T(8,128)(2,1)} %copy-done.18, bf16[576,512]{1,0:T(8,128)(2,1)} %copy-done.1, ...), custom_call_target="tpu_custom_call" | custom-call | flops 1000000000 | bytes 7735552 | tf_op jit(solution)/shard_map/pallas_call | solution.py:357
  147.7 0.7 slice_bitcast_fusion
  (86 shorter events, 3.5 us)
Async XLA Ops:
  6.1 8.9 %collective-permute-start = (bf16[288,512]{1,0:T(8,128)(2,1)}, bf16[288,512]{1,0:T(8,128)(2,1)S(1)}, u32[]{:S(2)}, u32[]{:S(2)}) collective-permute-start(bf16[288,512]{1,0:T(8,128)(2,1)} %get-tuple-element.34), channel_id=1, source_target_pairs={{0,15},{1,0},{2,1},{3,2},{4,3},{5,4},{6,5},{7,6},{8,7},{9,8},{10,9... | collective-permute-start | bytes 884744 | tf_op jit(solution)/shard_map/ppermute | solution.py:386
  6.4 6.5 %collective-permute-start.1 = (bf16[48,512]{1,0:T(8,128)(2,1)}, bf16[48,512]{1,0:T(8,128)(2,1)S(1)}, u32[]{:S(2)}, u32[]{:S(2)}) collective-permute-start(bf16[48,512]{1,0:T(8,128)(2,1)} %get-tuple-element.35), channel_id=1, source_target_pairs={{0,240},{16,0},{32,16},{48,32},{64,48},{80,64},{96,80},{112,96},{1... | collective-permute-start | bytes 147464 | tf_op jit(solution)/shard_map/ppermute | solution.py:386
  6.5 8.5 %collective-permute-start.2 = (bf16[48,512]{1,0:T(8,128)(2,1)}, bf16[48,512]{1,0:T(8,128)(2,1)S(1)}, u32[]{:S(2)}, u32[]{:S(2)}) collective-permute-start(bf16[48,512]{1,0:T(8,128)(2,1)} %get-tuple-element.36), channel_id=1, source_target_pairs={{0,255},{1,240},{2,241},{3,242},{4,243},{5,244},{6,245},{7,246},{8... | collective-permute-start | bytes 147464 | tf_op jit(solution)/shard_map/ppermute | solution.py:385
  15.0 1.4 copy-start.7
  17.8 1.0 copy-start.15
  23.9 12.5 %collective-permute-start.3 = (bf16[288,512]{1,0:T(8,128)(2,1)S(1)}, bf16[288,512]{1,0:T(8,128)(2,1)S(1)}, u32[]{:S(2)}, u32[]{:S(2)}) collective-permute-start(bf16[288,512]{1,0:T(8,128)(2,1)S(1)} %get-tuple-element.38), channel_id=1, source_target_pairs={{0,1},{1,2},{2,3},{3,4},{4,5},{5,6},{6,7},{7,8},{8,9},{9,10},{10,1... | collective-permute-start | bytes 884744 | tf_op jit(solution)/shard_map/ppermute | solution.py:386
  25.4 11.0 %collective-permute-start.4 = (bf16[48,512]{1,0:T(8,128)(2,1)S(1)}, bf16[48,512]{1,0:T(8,128)(2,1)S(1)}, u32[]{:S(2)}, u32[]{:S(2)}) collective-permute-start(bf16[48,512]{1,0:T(8,128)(2,1)S(1)} %get-tuple-element.39), channel_id=1, source_target_pairs={{0,16},{16,32},{32,48},{48,64},{64,80},{80,96},{96,112},{112,128},... | collective-permute-start | bytes 147464 | tf_op jit(solution)/shard_map/ppermute | solution.py:386
  27.3 9.0 %collective-permute-start.5 = (bf16[48,512]{1,0:T(8,128)(2,1)S(1)}, bf16[48,512]{1,0:T(8,128)(2,1)S(1)}, u32[]{:S(2)}, u32[]{:S(2)}) collective-permute-start(bf16[48,512]{1,0:T(8,128)(2,1)S(1)} %get-tuple-element.40), channel_id=1, source_target_pairs={{0,17},{1,18},{2,19},{3,20},{4,21},{5,22},{6,23},{7,24},{8,25},{9,... | collective-permute-start | bytes 147464 | tf_op jit(solution)/shard_map/ppermute | solution.py:385
  29.0 7.3 %copy-start.19 = (bf16[2048]{0:T(1024)(128)(2,1)S(1)}, bf16[2048]{0:T(1024)(128)(2,1)}, u32[]{:S(2)}) copy-start(bf16[2048]{0:T(1024)(128)(2,1)} %param.30) | copy-start | bytes 12292
  29.0 7.3 %copy-start.20 = (bf16[1024]{0:T(1024)(128)(2,1)S(1)}, bf16[1024]{0:T(1024)(128)(2,1)}, u32[]{:S(2)}) copy-start(bf16[1024]{0:T(1024)(128)(2,1)} %param.32) | copy-start | bytes 6148
  29.0 7.4 %copy-start.8 = (bf16[512,512]{1,0:T(8,128)(2,1)S(1)}, bf16[512,512]{1,0:T(8,128)(2,1)}, u32[]{:S(2)}) copy-start(bf16[512,512]{1,0:T(8,128)(2,1)} %w_proj.1) | copy-start | bytes 1572868
  29.0 7.4 %copy-start.13 = (s32[1,96]{1,0:T(1,128)S(1)}, s32[1,96]{1,0:T(1,128)}, u32[]{:S(2)}) copy-start(s32[1,96]{1,0:T(1,128)} %constant.46.clone.e2m) | copy-start | bytes 1156
  29.0 7.4 %copy-start.14 = (f32[576,512]{1,0:T(8,128)S(1)}, f32[576,512]{1,0:T(8,128)}, u32[]{:S(2)}) copy-start(f32[576,512]{1,0:T(8,128)} %get-tuple-element.41.fields) | copy-start | bytes 3538948
  34.2 10.0 %collective-permute-start.23 = (bf16[144,1024]{1,0:T(8,128)(2,1)}, bf16[144,1024]{1,0:T(8,128)(2,1)S(1)}, u32[]{:S(2)}, u32[]{:S(2)}) collective-permute-start(bf16[144,1024]{1,0:T(8,128)(2,1)} %shard_map.237.own), channel_id=1, source_target_pairs={{0,2},{1,3},{2,4},{3,5},{4,6},{5,7},{6,0},{7,1},{8,10},{9,11},{10,... | collective-permute-start | bytes 884744 | tf_op jit(solution)/shard_map/ppermute | solution.py:377
  34.3 10.8 %collective-permute-start.24 = (bf16[144,1024]{1,0:T(8,128)(2,1)}, bf16[144,1024]{1,0:T(8,128)(2,1)S(1)}, u32[]{:S(2)}, u32[]{:S(2)}) collective-permute-start(bf16[144,1024]{1,0:T(8,128)(2,1)} %shard_map.237.own), channel_id=1, source_target_pairs={{0,6},{1,7},{2,0},{3,1},{4,2},{5,3},{6,4},{7,5},{8,14},{9,15},{10,... | collective-permute-start | bytes 884744 | tf_op jit(solution)/shard_map/ppermute | solution.py:377
  36.4 2.2 %copy-start.6 = (bf16[2048,1024]{1,0:T(8,128)(2,1)S(1)}, bf16[2048,1024]{1,0:T(8,128)(2,1)}, u32[]{:S(2)}) copy-start(bf16[2048,1024]{1,0:T(8,128)(2,1)} %w_merge.1) | copy-start | bytes 12582916
  38.6 5.6 %copy-start.9 = (bf16[1024,256]{1,0:T(8,128)(2,1)S(1)}, bf16[1024,256]{1,0:T(8,128)(2,1)}, u32[]{:S(2)}) copy-start(bf16[1024,256]{1,0:T(8,128)(2,1)} %w_in.3) | copy-start | bytes 1572868
  38.6 6.5 %copy-start.10 = (bf16[256,1024]{1,0:T(8,128)(2,1)S(1)}, bf16[256,1024]{1,0:T(8,128)(2,1)}, u32[]{:S(2)}) copy-start(bf16[256,1024]{1,0:T(8,128)(2,1)} %w_out.5) | copy-start | bytes 1572868
  40.5 18.0 %copy-start.1 = (bf16[576,512]{1,0:T(8,128)(2,1)}, bf16[576,512]{1,0:T(8,128)(2,1)S(1)}, u32[]{:S(2)}) copy-start(bf16[576,512]{1,0:T(8,128)(2,1)S(1)} %get-tuple-element.52.skip) | copy-start | bytes 1769476
  40.5 18.0 %copy-start.4 = (bf16[144,1024]{1,0:T(8,128)(2,1)}, bf16[144,1024]{1,0:T(8,128)(2,1)S(1)}, u32[]{:S(2)}) copy-start(bf16[144,1024]{1,0:T(8,128)(2,1)S(1)} %get-tuple-element.42.coarse) | copy-start | bytes 884740
  40.5 9.4 %collective-permute-start.7 = (bf16[144,1024]{1,0:T(8,128)(2,1)S(1)}, bf16[144,1024]{1,0:T(8,128)(2,1)S(1)}, u32[]{:S(2)}, u32[]{:S(2)}) collective-permute-start(bf16[144,1024]{1,0:T(8,128)(2,1)S(1)} %get-tuple-element.43.own), channel_id=1, source_target_pairs={{0,2},{1,3},{2,4},{3,5},{4,6},{5,7},{6,0},{7,1},{8,10},{9,11},{10,... | collective-permute-start | bytes 884744 | tf_op jit(solution)/shard_map/ppermute | solution.py:377
  42.1 10.1 %collective-permute-start.6 = (bf16[144,1024]{1,0:T(8,128)(2,1)S(1)}, bf16[144,1024]{1,0:T(8,128)(2,1)S(1)}, u32[]{:S(2)}, u32[]{:S(2)}) collective-permute-start(bf16[144,1024]{1,0:T(8,128)(2,1)S(1)} %get-tuple-element.43.own), channel_id=1, source_target_pairs={{0,8},{1,9},{2,10},{3,11},{4,12},{5,13},{6,14},{7,15},{8,0},{9,1},... | collective-permute-start | bytes 884744 | tf_op jit(solution)/shard_map/ppermute | solution.py:377
  43.8 8.9 %collective-permute-start.8 = (bf16[144,1024]{1,0:T(8,128)(2,1)S(1)}, bf16[144,1024]{1,0:T(8,128)(2,1)S(1)}, u32[]{:S(2)}, u32[]{:S(2)}) collective-permute-start(bf16[144,1024]{1,0:T(8,128)(2,1)S(1)} %get-tuple-element.43.own), channel_id=1, source_target_pairs={{0,6},{1,7},{2,0},{3,1},{4,2},{5,3},{6,4},{7,5},{8,14},{9,15},{10,... | collective-permute-start | bytes 884744 | tf_op jit(solution)/shard_map/ppermute | solution.py:377
  44.2 25.2 %collective-permute-start.9 = (bf16[1024,256]{1,0:T(8,128)(2,1)S(1)}, bf16[1024,256]{1,0:T(8,128)(2,1)S(1)}, u32[]{:S(2)}, u32[]{:S(2)}) collective-permute-start(bf16[1024,256]{1,0:T(8,128)(2,1)S(1)} %copy-done.9), channel_id=1, source_target_pairs={{0,1},{1,0},{2,3},{3,2},{4,5},{5,4},{6,7},{7,6},{8,9},{9,8},{10,11... | collective-permute-start | bytes 1572872 | tf_op jit(solution)/shard_map/ppermute | solution.py:377
  45.1 27.8 %collective-permute-start.10 = (bf16[256,1024]{1,0:T(8,128)(2,1)S(1)}, bf16[256,1024]{1,0:T(8,128)(2,1)S(1)}, u32[]{:S(2)}, u32[]{:S(2)}) collective-permute-start(bf16[256,1024]{1,0:T(8,128)(2,1)S(1)} %copy-done.10), channel_id=1, source_target_pairs={{0,1},{1,0},{2,3},{3,2},{4,5},{5,4},{6,7},{7,6},{8,9},{9,8},{10,11... | collective-permute-start | bytes 1572872 | tf_op jit(solution)/shard_map/ppermute | solution.py:377
  50.0 8.5 %collective-permute-start.25 = (bf16[80,1024]{1,0:T(8,128)(2,1)S(1)}, bf16[80,1024]{1,0:T(8,128)(2,1)S(1)}, u32[]{:S(2)}, u32[]{:S(2)}) collective-permute-start(bf16[80,1024]{1,0:T(8,128)(2,1)S(1)} %slice.36), channel_id=1, source_target_pairs={{0,2},{1,3},{2,4},{3,5},{4,6},{5,7},{6,0},{7,1},{8,10},{9,11},{10,... | collective-permute-start | bytes 491528 | tf_op jit(solution)/shard_map/ppermute | solution.py:377
  52.2 16.9 %copy-start.5 = (bf16[144,1024]{1,0:T(8,128)(2,1)S(1)}, bf16[144,1024]{1,0:T(8,128)(2,1)}, u32[]{:S(2)}) copy-start(bf16[144,1024]{1,0:T(8,128)(2,1)} %shard_map.237.own) | copy-start | bytes 884740
  52.2 6.3 %collective-permute-start.26 = (bf16[64,1024]{1,0:T(8,128)(2,1)S(1)}, bf16[64,1024]{1,0:T(8,128)(2,1)S(1)}, u32[]{:S(2)}, u32[]{:S(2)}) collective-permute-start(bf16[64,1024]{1,0:T(8,128)(2,1)S(1)} %slice.37), channel_id=1, source_target_pairs={{0,6},{1,7},{2,0},{3,1},{4,2},{5,3},{6,4},{7,5},{8,14},{9,15},{10,... | collective-permute-start | bytes 393224 | tf_op jit(solution)/shard_map/ppermute | solution.py:377
  52.7 16.6 %collective-permute-start.11 = (bf16[224,1024]{1,0:T(8,128)(2,1)S(1)}, bf16[224,1024]{1,0:T(8,128)(2,1)S(1)}, u32[]{:S(2)}, u32[]{:S(2)}) collective-permute-start(bf16[224,1024]{1,0:T(8,128)(2,1)S(1)} %pad_maximum_fusion.1), channel_id=1, source_target_pairs={{0,2},{1,3},{2,4},{3,5},{4,6},{5,7},{6,0},{7,1},{8,10},{9,11},{10,... | collective-permute-start | bytes 1376264 | tf_op jit(solution)/shard_map/ppermute | solution.py:377
  58.4 10.6 %collective-permute-start.12 = (bf16[208,1024]{1,0:T(8,128)(2,1)S(1)}, bf16[208,1024]{1,0:T(8,128)(2,1)S(1)}, u32[]{:S(2)}, u32[]{:S(2)}) collective-permute-start(bf16[208,1024]{1,0:T(8,128)(2,1)S(1)} %pad_maximum_fusion.2), channel_id=1, source_target_pairs={{0,6},{1,7},{2,0},{3,1},{4,2},{5,3},{6,4},{7,5},{8,14},{9,15},{10,... | collective-permute-start | bytes 1277960 | tf_op jit(solution)/shard_map/ppermute | solution.py:377
  58.5 27.1 %collective-permute-start.27 = (bf16[432,1024]{1,0:T(8,128)(2,1)S(1)}, bf16[432,1024]{1,0:T(8,128)(2,1)S(1)}, u32[]{:S(2)}, u32[]{:S(2)}) collective-permute-start(bf16[432,1024]{1,0:T(8,128)(2,1)S(1)} %pad_maximum_fusion), channel_id=1, source_target_pairs={{0,8},{1,9},{2,10},{3,11},{4,12},{5,13},{6,14},{7,15},{8,0},{9,1},... | collective-permute-start | bytes 2654216 | tf_op jit(solution)/shard_map/ppermute | solution.py:377
  69.0 16.6 %collective-permute-start.22 = (bf16[144,1024]{1,0:T(8,128)(2,1)S(1)}, bf16[144,1024]{1,0:T(8,128)(2,1)S(1)}, u32[]{:S(2)}, u32[]{:S(2)}) collective-permute-start(bf16[144,1024]{1,0:T(8,128)(2,1)S(1)} %copy-done.5), channel_id=1, source_target_pairs={{0,8},{1,9},{2,10},{3,11},{4,12},{5,13},{6,14},{7,15},{8,0},{9,1},... | collective-permute-start | bytes 884744 | tf_op jit(solution)/shard_map/ppermute | solution.py:377
  69.3 6.3 %collective-permute-start.14 = (bf16[64,1024]{1,0:T(8,128)(2,1)S(1)}, bf16[64,1024]{1,0:T(8,128)(2,1)S(1)}, u32[]{:S(2)}, u32[]{:S(2)}) collective-permute-start(bf16[64,1024]{1,0:T(8,128)(2,1)S(1)} %slice.35), channel_id=1, source_target_pairs={{0,6},{1,7},{2,0},{3,1},{4,2},{5,3},{6,4},{7,5},{8,14},{9,15},{10,... | collective-permute-start | bytes 393224 | tf_op jit(solution)/shard_map/ppermute | solution.py:377
  69.4 6.4 %collective-permute-start.13 = (bf16[80,1024]{1,0:T(8,128)(2,1)S(1)}, bf16[80,1024]{1,0:T(8,128)(2,1)S(1)}, u32[]{:S(2)}, u32[]{:S(2)}) collective-permute-start(bf16[80,1024]{1,0:T(8,128)(2,1)S(1)} %slice.34), channel_id=1, source_target_pairs={{0,2},{1,3},{2,4},{3,5},{4,6},{5,7},{6,0},{7,1},{8,10},{9,11},{10,... | collective-permute-start | bytes 491528 | tf_op jit(solution)/shard_map/ppermute | solution.py:377
  75.3 57.3 %copy-start = (bf16[576,1024]{1,0:T(8,128)(2,1)}, bf16[576,1024]{1,0:T(8,128)(2,1)S(1)}, u32[]{:S(2)}) copy-start(bf16[576,1024]{1,0:T(8,128)(2,1)S(1)} %get-tuple-element.44.near) | copy-start | bytes 3538948
  92.2 2.9 %collective-permute-start.28 = (bf16[2048,256]{1,0:T(8,128)(2,1)}, bf16[2048,256]{1,0:T(8,128)(2,1)S(1)}, u32[]{:S(2)}, u32[]{:S(2)}) collective-permute-start(bf16[2048,256]{1,0:T(8,128)(2,1)} %get-tuple-element.60), channel_id=1, source_target_pairs={{0,1},{1,0},{2,3},{3,2},{4,5},{5,4},{6,7},{7,6},{8,9},{9,8},{10,11... | collective-permute-start | bytes 3145736 | tf_op jit(solution)/shard_map/ppermute | solution.py:377
  95.3 23.1 %copy-start.3 = (bf16[288,1024]{1,0:T(8,128)(2,1)S(1)}, bf16[288,1024]{1,0:T(8,128)(2,1)}, u32[]{:S(2)}) copy-start(bf16[288,1024]{1,0:T(8,128)(2,1)} %copy-done.2) | copy-start | bytes 1769476
  95.3 14.1 %collective-permute-start.29 = (bf16[1024,256]{1,0:T(8,128)(2,1)S(1)}, bf16[1024,256]{1,0:T(8,128)(2,1)S(1)}, u32[]{:S(2)}, u32[]{:S(2)}) collective-permute-start(bf16[1024,256]{1,0:T(8,128)(2,1)S(1)} %get-tuple-element.62), channel_id=1, source_target_pairs={{0,128},{16,144},{32,160},{48,176},{64,192},{80,208},{96,224},{112... | collective-permute-start | bytes 1572872 | tf_op jit(solution)/shard_map/ppermute | solution.py:478
  96.6 21.7 %collective-permute-start.15 = (bf16[160,1024]{1,0:T(8,128)(2,1)}, bf16[160,1024]{1,0:T(8,128)(2,1)S(1)}, u32[]{:S(2)}, u32[]{:S(2)}) collective-permute-start(bf16[160,1024]{1,0:T(8,128)(2,1)} %get-tuple-element.46), channel_id=1, source_target_pairs={{0,2},{1,3},{2,4},{3,5},{4,6},{5,7},{6,0},{7,1},{8,10},{9,11},{10,... | collective-permute-start | bytes 983048 | tf_op jit(solution)/shard_map/ppermute | solution.py:377
  99.6 18.8 %collective-permute-start.16 = (bf16[128,1024]{1,0:T(8,128)(2,1)S(1)}, bf16[128,1024]{1,0:T(8,128)(2,1)S(1)}, u32[]{:S(2)}, u32[]{:S(2)}) collective-permute-start(bf16[128,1024]{1,0:T(8,128)(2,1)S(1)} %get-tuple-element.47), channel_id=1, source_target_pairs={{0,6},{1,7},{2,0},{3,1},{4,2},{5,3},{6,4},{7,5},{8,14},{9,15},{10,... | collective-permute-start | bytes 786440 | tf_op jit(solution)/shard_map/ppermute | solution.py:377
  110.3 37.4 %all-to-all-start = ((bf16[8,128,256]{2,1,0:T(8,128)(2,1)}), bf16[8,128,256]{2,1,0:T(8,128)(2,1)S(1)}, u32[]{:S(2)}, u32[]{:S(2)}) async-start(bf16[8,128,256]{2,1,0:T(8,128)(2,1)} %bitcast.5), calls=%async_computation | async-start | bytes 1048576 | tf_op jit(solution)/shard_map/all_to_all | solution.py:480
  118.5 10.4 %collective-permute-start.19 = (bf16[144,1024]{1,0:T(8,128)(2,1)S(1)}, bf16[144,1024]{1,0:T(8,128)(2,1)S(1)}, u32[]{:S(2)}, u32[]{:S(2)}) collective-permute-start(bf16[144,1024]{1,0:T(8,128)(2,1)S(1)} %get-tuple-element.50), channel_id=1, source_target_pairs={{0,2},{1,3},{2,4},{3,5},{4,6},{5,7},{6,0},{7,1},{8,10},{9,11},{10,... | collective-permute-start | bytes 884744 | tf_op jit(solution)/shard_map/ppermute | solution.py:377
  121.6 11.1 %collective-permute-start.20 = (bf16[144,1024]{1,0:T(8,128)(2,1)S(1)}, bf16[144,1024]{1,0:T(8,128)(2,1)S(1)}, u32[]{:S(2)}, u32[]{:S(2)}) collective-permute-start(bf16[144,1024]{1,0:T(8,128)(2,1)S(1)} %get-tuple-element.51), channel_id=1, source_target_pairs={{0,6},{1,7},{2,0},{3,1},{4,2},{5,3},{6,4},{7,5},{8,14},{9,15},{10,... | collective-permute-start | bytes 884744 | tf_op jit(solution)/shard_map/ppermute | solution.py:377
  121.6 11.6 %collective-permute-start.17 = (bf16[144,1024]{1,0:T(8,128)(2,1)S(1)}, bf16[144,1024]{1,0:T(8,128)(2,1)S(1)}, u32[]{:S(2)}, u32[]{:S(2)}) collective-permute-start(bf16[144,1024]{1,0:T(8,128)(2,1)S(1)} %get-tuple-element.48), channel_id=1, source_target_pairs={{0,2},{1,3},{2,4},{3,5},{4,6},{5,7},{6,0},{7,1},{8,10},{9,11},{10,... | collective-permute-start | bytes 884744 | tf_op jit(solution)/shard_map/ppermute | solution.py:377
  124.8 11.6 %collective-permute-start.18 = (bf16[144,1024]{1,0:T(8,128)(2,1)S(1)}, bf16[144,1024]{1,0:T(8,128)(2,1)S(1)}, u32[]{:S(2)}, u32[]{:S(2)}) collective-permute-start(bf16[144,1024]{1,0:T(8,128)(2,1)S(1)} %get-tuple-element.49), channel_id=1, source_target_pairs={{0,6},{1,7},{2,0},{3,1},{4,2},{5,3},{6,4},{7,5},{8,14},{9,15},{10,... | collective-permute-start | bytes 884744 | tf_op jit(solution)/shard_map/ppermute | solution.py:377
  132.8 8.3 %collective-permute-start.21 = (bf16[144,1024]{1,0:T(8,128)(2,1)S(1)}, bf16[144,1024]{1,0:T(8,128)(2,1)S(1)}, u32[]{:S(2)}, u32[]{:S(2)}) collective-permute-start(bf16[144,1024]{1,0:T(8,128)(2,1)S(1)} %shard_map.235), channel_id=1, source_target_pairs={{0,8},{1,9},{2,10},{3,11},{4,12},{5,13},{6,14},{7,15},{8,0},{9,1},... | collective-permute-start | bytes 884744 | tf_op jit(solution)/shard_map/ppermute | solution.py:377
  133.2 7.9 %copy-start.16 = (bf16[144,1024]{1,0:T(8,128)(2,1)}, bf16[144,1024]{1,0:T(8,128)(2,1)S(1)}, u32[]{:S(2)}) copy-start(bf16[144,1024]{1,0:T(8,128)(2,1)S(1)} %collective-permute-done.17.got_right) | copy-start | bytes 884740
  136.5 4.6 %copy-start.17 = (bf16[144,1024]{1,0:T(8,128)(2,1)}, bf16[144,1024]{1,0:T(8,128)(2,1)S(1)}, u32[]{:S(2)}) copy-start(bf16[144,1024]{1,0:T(8,128)(2,1)S(1)} %collective-permute-done.18.got_left) | copy-start | bytes 884740
  (4 other events, 2.9 us)
